TPU v7x, 128 devices: a whole 4x4x4 slice. The times are simulated.
128 devices in a mesh: shot: 4 (over y_hi, core), gx: 8 (over y_lo, z), gy: 4 (over x).
Axes of the slice: x: 4, y: 4 (y_hi: 2, y_lo: 2; y = y_hi * 2 + y_lo), z: 4, core: 2. Of those that a mesh axis runs over, the one named last changes fastest.
Arguments:
- state_now: float32 [4, 64, 256, 256], P('shot', 'gx', 'gy'), may hold values from -6 to 6
- state_prev: float32 [4, 64, 256, 256], P('shot', 'gx', 'gy'), may hold values from -6 to 6
- courant_sq: float32 [64, 256, 256], P('gx', 'gy'), may hold values from 0.03 to 0.3
- reflectivity: float32 [64, 256, 256], P('gx', 'gy'), may hold values from -6 to 6
- direction: float32 [64, 256, 256], P('gx', 'gy'), may hold values from -6 to 6
- prev_gradient: float32 [64, 256, 256], P('gx', 'gy'), may hold values from -3 to 3
- residual: float32 [4, 16, 64, 256], P('shot', None, 'gx', 'gy'), may hold values from -6 to 6
- rec_depth: int32 [4, 64, 256], P('shot', 'gx', 'gy'), may hold values from 0 to 255
- source_cell: int32 [4, 3], P('shot'), may hold values from 0 to 255, as said below
- wavelet: float32 [4, 15], P('shot'), may hold values from -80 to 80
- live_steps: int32 [4], P('shot'), may hold values from 8 to 16
Outputs:
- image_next: float32 [64, 256, 256], P('gx', 'gy')
- direction_next: float32 [64, 256, 256], P('gx', 'gy')
- residual_next: float32 [4, 16, 64, 256], P('shot', None, 'gx', 'gy')
- data_misfit: float32 [], replicated
Inputs may be any that keep to these rules, and one draw needn't show every extreme that they name: `source_cell`: column 0 lies in 0 to 63, column 1 in 0 to 255, column 2 in 0 to 255.
All inputs are finite; a program needn't handle non-finite values.
Results may differ from a plain program's by a relative error of at most 0.0003.
Values sent between devices are 32-bit elements; how exact they have to be, the bound alone decides.
A program may use at most 64 MiB of HBM per device.

v0:
```python
import jax
import jax.numpy as jnp
from jax import lax
from jax.sharding import Mesh
from jax.sharding import PartitionSpec as P

GX = ("gx_0", "gx_1")
SHOT = ("shot_0", "shot_1")
SHOT_GX_GY = ("shot_0", "shot_1", "gx_0", "gx_1", "gy")


def with_halo(array, sides, width):
    edges = {}
    for axis, dim in sides:
        size, length = (lax.axis_size(axis), array.shape[dim])
        up = [(i, (i + 1) % size) for i in range(size - 1)]
        last = lax.slice_in_dim(array, length - width, length, axis=dim)
        first = lax.slice_in_dim(array, 0, width, axis=dim)
        edges[dim] = (
            lax.ppermute(last, axis, up),
            lax.ppermute(first, axis, [(b, a) for a, b in up]),
        )
    done = []
    for _, dim in sides:
        low, high = edges[dim]
        around = [(width, width) if d in done else (0, 0) for d in range(array.ndim)]
        array = jnp.concatenate([jnp.pad(low, around), array, jnp.pad(high, around)], axis=dim)
        done.append(dim)
    return array


def copy_for_each(array, axis):
    copies = jnp.broadcast_to(array, (lax.axis_size(axis), *array.shape))
    return lax.all_to_all(copies, axis, split_axis=0, concat_axis=0, tiled=True)


def of_everyone(array, axis):
    everything = copy_for_each(array, axis)
    return jnp.sum(everything, axis=0)


def over_axes(array, axes):
    for axis in axes:
        array = lax.psum(array, axis)
    return array


def neighbours(padded, values):
    inner = padded[:, 2:, 1:-1] + padded[:, :-2, 1:-1] + padded[:, 1:-1, 2:] + padded[:, 1:-1, :-2]
    deeper = jnp.pad(values, ((0, 0), (0, 0), (0, 0), (1, 1)))
    inner = inner + deeper[:, :, :, 2:] + deeper[:, :, :, :-2]
    return inner - 6.0 * values


def on_device(
    state_now,
    state_prev,
    courant_sq,
    reflectivity,
    direction,
    prev_gradient,
    residual,
    rec_depth,
    source_cell,
    wavelet,
    live_steps,
):
    shot_count, extent_x, extent_y, extent_z = state_now.shape
    step_count = residual.shape[1]
    global_x = lax.axis_index(GX) * extent_x + lax.iota(jnp.int32, extent_x)
    global_y = lax.axis_index("gy") * extent_y + lax.iota(jnp.int32, extent_y)
    depth_axis = lax.iota(jnp.int32, extent_z)
    spot = (
        (global_x[None, :, None, None] == source_cell[:, 0, None, None, None])
        & (global_y[None, None, :, None] == source_cell[:, 1, None, None, None])
        & (depth_axis[None, None, None, :] == source_cell[:, 2, None, None, None])
    ).astype(jnp.float32)
    receivers = (depth_axis[None, None, None, :] == rec_depth[:, :, :, None]).astype(jnp.float32)
    live_mask = (lax.iota(jnp.int32, step_count)[None, :] < live_steps[:, None]).astype(jnp.float32)
    weighted = residual * live_mask[:, :, None, None]
    stored = jnp.zeros((step_count,) + state_now.shape, jnp.float32)
    stored = lax.dynamic_update_index_in_dim(stored, state_now, 0, 0)

    def advance(index, carry):
        present, former, history = carry
        padded = with_halo(present, ((GX, 1), ("gy", 2)), 1)
        amplitude = lax.dynamic_index_in_dim(wavelet, index, 1, keepdims=False)
        advanced = (
            2.0 * present
            - former
            + courant_sq * neighbours(padded, present)
            + amplitude[:, None, None, None] * spot
        )
        history = lax.dynamic_update_index_in_dim(history, advanced, index + 1, 0)
        return (advanced, present, history)

    unused_a, unused_b, stored = lax.fori_loop(
        0, step_count - 1, advance, (state_now, state_prev, stored)
    )
    newest = receivers * weighted[:, step_count - 1, :, :, None]
    accumulated = stored[step_count - 1] * newest

    def retreat(offset, carry):
        following, furthest, summed = carry
        index = step_count - 2 - offset
        scaled = courant_sq * following
        padded = with_halo(scaled, ((GX, 1), ("gy", 2)), 1)
        weight = lax.dynamic_index_in_dim(weighted, index, 1, keepdims=False)
        current = (
            2.0 * following
            - furthest
            + neighbours(padded, scaled)
            + receivers * weight[:, :, :, None]
        )
        wavefield = lax.dynamic_index_in_dim(stored, index, 0, keepdims=False)
        return (current, following, summed + wavefield * current)

    unused_c, unused_d, accumulated = lax.fori_loop(
        0, step_count - 1, retreat, (newest, jnp.zeros_like(newest), accumulated)
    )
    local_gradient = courant_sq * jnp.sum(accumulated, axis=0)
    quarter = extent_z // lax.axis_size(SHOT)
    offset_z = lax.axis_index(SHOT) * quarter

    def share(values):
        return lax.dynamic_slice_in_dim(values, offset_z, quarter, 2)

    gradient = of_everyone(local_gradient, SHOT)
    grad_share = share(gradient)
    old_share = share(prev_gradient)
    path_share = share(direction)
    partials = (
        jnp.sum(grad_share * grad_share),
        jnp.sum(grad_share * old_share),
        jnp.sum(old_share * old_share),
    )
    partials = partials + (jnp.sum(grad_share * path_share),)
    summed = jax.tree.map(lambda part: over_axes(part, SHOT_GX_GY), partials)
    beta_coef = (summed[0] - summed[1]) / summed[2]
    direction_next = gradient + beta_coef * direction
    slope = summed[0] + beta_coef * summed[3]
    gain = courant_sq * direction_next
    first_wave = gain * stored[0]
    records = jnp.zeros(residual.shape, jnp.float32)
    first_record = jnp.sum(receivers * first_wave, axis=3) * live_mask[:, 0, None, None]
    records = lax.dynamic_update_index_in_dim(records, first_record, 0, 1)

    def propagate(index, carry):
        present, former, gathered = carry
        padded = with_halo(present, ((GX, 1), ("gy", 2)), 1)
        wavefield = lax.dynamic_index_in_dim(stored, index, 0, keepdims=False)
        advanced = (
            2.0 * present - former + courant_sq * neighbours(padded, present) + gain * wavefield
        )
        live_now = lax.dynamic_index_in_dim(live_mask, index, 1, keepdims=False)
        sampled = jnp.sum(receivers * advanced, axis=3) * live_now[:, None, None]
        gathered = lax.dynamic_update_index_in_dim(gathered, sampled, index, 1)
        return (advanced, present, gathered)

    unused_e, unused_f, records = lax.fori_loop(
        1, step_count, propagate, (first_wave, jnp.zeros_like(first_wave), records)
    )
    partials = (jnp.sum(records * records),)
    partials = partials + (jnp.sum(residual * records), jnp.sum(residual * residual))
    totals = jax.tree.map(lambda part: over_axes(part, SHOT_GX_GY), partials)
    step_length = slope / totals[0]
    image_next = reflectivity + step_length * direction_next
    residual_next = residual - step_length * records
    entry_count = float(
        shot_count
        * step_count
        * extent_x
        * extent_y
        * lax.axis_size(SHOT)
        * lax.axis_size(GX)
        * lax.axis_size("gy")
    )
    misfit_sum = totals[2] - 2.0 * step_length * totals[1] + step_length * step_length * totals[0]
    return (image_next, direction_next, residual_next, 0.5 * misfit_sum / entry_count)


def solution(mesh):
    finer = Mesh(
        mesh.devices.reshape(2, 2, 2, 4, mesh.shape["gy"]),
        ("shot_0", "shot_1", "gx_0", "gx_1", "gy"),
    )
    placed = (
        P(SHOT, GX, "gy", None),
        P(SHOT, GX, "gy", None),
        P(GX, "gy", None),
        P(GX, "gy", None),
        P(GX, "gy", None),
        P(GX, "gy", None),
        P(SHOT, None, GX, "gy"),
        P(SHOT, GX, "gy"),
        P(SHOT, None),
        P(SHOT, None),
        P(SHOT),
    )
    return jax.shard_map(
        on_device,
        mesh=finer,
        in_specs=placed,
        out_specs=(P(GX, "gy", None), P(GX, "gy", None), P(SHOT, None, GX, "gy"), P()),
        check_vma=False,
    )
```

profile of v0, /device:TPU:1, one launch (start us, length us, event | category | flops | bytes accessed | tf_op | source)
XLA Modules:
  0.0 923.1 jit_solution(311010648920365051)
XLA Ops:
  11.2 232.1 %while.62 = (s32[]{:T(128)}, f32[1,8,64,256]{3,2,1,0:T(8,128)S(1)}, f32[1,8,64,256]{3,2,1,0:T(8,128)S(1)}, f32[16,1,8,64,256]{4,3,2,1,0:T(8,128)}, f32[8,64,256]...) while((s32[]{:T(128)}, f32[1,8,64,256]{3,2,1,0:T(8,128)S(1)}, ...), condition=%wide.region_1.2_spmd.clone, body=%wide.region_0.1_spmd.clone.sunk | while | flops 3145733 | bytes 7718471 | solution.py:97
  84.4 6.1 collective-permute-start
  100.3 6.1 collective-permute-start
  116.4 6.4 collective-permute-start
  148.1 6.1 collective-permute-start
  211.6 6.4 collective-permute-start
  244.6 236.1 %while.63 = (s32[]{:T(128)}, f32[1,8,64,256]{3,2,1,0:T(8,128)S(1)}, f32[1,8,64,256]{3,2,1,0:T(8,128)S(1)}, f32[1,8,64,256]{3,2,1,0:T(8,128)S(1)}, f32[8,64,256]{...) while((s32[]{:T(128)}, f32[1,8,64,256]{3,2,1,0:T(8,128)S(1)}, ...), condition=%wide.region_3.4_spmd.clone, body=%wide.region_2.3_spmd.clone.sunk | while | flops 3932166 | bytes 8380747 | solution.py:118
  246.0 6.7 collective-permute-start.5
  293.6 6.2 collective-permute-start.5
  403.7 6.1 collective-permute-start.5
  419.4 6.1 collective-permute-start.5
  482.4 55.1 %all-to-all-start = ((f32[4,8,64,256]{3,2,1,0:T(8,128)}), f32[4,8,64,256]{3,2,1,0:T(8,128)S(1)}, u32[]{:S(2)}, u32[]{:S(2)}) async-start(f32[4,8,64,256]{3,2,1,0:T(8,128)} %broadcast_in_dim.80), calls=%async_computation | async-start | bytes 4194304 | tf_op jit(solution)/shard_map/all_to_all | solution.py:34
  537.5 26.2 %all-to-all-done = f32[4,8,64,256]{3,2,1,0:T(8,128)S(1)} async-done(((f32[4,8,64,256]{3,2,1,0:T(8,128)}), f32[4,8,64,256]{3,2,1,0:T(8,128)S(1)}, u32[]{:S(2)}, u32[]{:S(2)}) %all-to-all-start) | async-done | bytes 2097184 | tf_op jit(solution)/shard_map/all_to_all | solution.py:34
  576.6 10.3 %all-reduce.16 = (f32[]{:T(128)}, f32[]{:T(128)}, f32[]{:T(128)}) all-reduce(f32[]{:T(128)} %get-tuple-element.811, f32[]{:T(128)} %get-tuple-element.812, f32[]{:T(128)} %get-tuple-element.813), channel_id=1, replica_groups=mesh['shot_0'=2,'shot_1'=2,'gx_0'=2,'gx_1'=4,'gy'=4] {'gx_0'}, use_global_device_ids=true, to_apply=%region_8.9 | all-reduce | flops 3 | bytes 24 | tf_op jit(solution)/shard_map/psum | solution.py:44
  586.9 11.3 %all-reduce.14 = (f32[]{:T(128)}, f32[]{:T(128)}, f32[]{:T(128)}) all-reduce(f32[]{:T(128)} %get-tuple-element.804, f32[]{:T(128)} %get-tuple-element.805, f32[]{:T(128)} %get-tuple-element.806), channel_id=1, replica_groups=mesh['shot_0'=2,'shot_1'=2,'gx_0'=2,'gx_1'=4,'gy'=4] {'gx_1'}, use_global_device_ids=true, to_apply=%region_9.10 | all-reduce | flops 3 | bytes 24 | tf_op jit(solution)/shard_map/psum | solution.py:44
  598.3 6.6 all-reduce.12
  610.2 235.9 %while.64 = (s32[]{:T(128)}, f32[1,8,64,256]{3,2,1,0:T(8,128)S(1)}, f32[1,8,64,256]{3,2,1,0:T(8,128)S(1)}, f32[1,16,8,64]{3,2,1,0:T(8,128)S(1)}, f32[8,64,256]{2...) while((s32[]{:T(128)}, f32[1,8,64,256]{3,2,1,0:T(8,128)S(1)}, ...), condition=%wide.region_32.33_spmd.clone, body=%wide.region_30.32_spmd.clone.sunk | while | flops 3407877 | bytes 8253783 | solution.py:160
  682.5 6.6 collective-permute-start.8
  731.7 6.4 collective-permute-start.8
  748.0 6.7 collective-permute-start.8
  852.7 34.0 %all-reduce.17 = (f32[]{:T(128)}, f32[]{:T(128)}, f32[]{:T(128)}, f32[]{:T(128)}) all-reduce(f32[]{:T(128)} %get-tuple-element.814, f32[]{:T(128)} %get-tuple-element.815, f32[]{:T(128)} %get-tuple-element.816, f32[]{:T(128)} %get-tuple-element.817), channel_id=1, replica_groups=mesh['shot_0'=2,'shot_1'=2,'gx_0'=2,'gx_1'=4,'gy'=4] {'shot_1'}, use_global_device_ids=true, to_apply=%region_25.26 | all-reduce | flops 4 | bytes 32 | tf_op jit(solution)/shard_map/psum | solution.py:44
  886.6 15.7 %all-reduce.15 = (f32[]{:T(128)}, f32[]{:T(128)}, f32[]{:T(128)}, f32[]{:T(128)}) all-reduce(f32[]{:T(128)} %get-tuple-element.807, f32[]{:T(128)} %get-tuple-element.808, f32[]{:T(128)} %get-tuple-element.809, f32[]{:T(128)} %get-tuple-element.810), channel_id=1, replica_groups=mesh['shot_0'=2,'shot_1'=2,'gx_0'=2,'gx_1'=4,'gy'=4] {'gx_0'}, use_global_device_ids=true, to_apply=%region_26.27 | all-reduce | flops 4 | bytes 32 | tf_op jit(solution)/shard_map/psum | solution.py:44
  902.4 6.7 all-reduce.13
  909.1 6.6 all-reduce.11
  (778 shorter events, 661.1 us)
Async XLA Ops:
  244.7 14.4 %collective-permute-start.4 = (f32[1,1,64,256]{3,2,1,0:T(8,128)S(1)}, f32[1,1,64,256]{3,2,1,0:T(8,128)S(1)}, u32[]{:S(2)}, u32[]{:S(2)}) collective-permute-start(f32[1,1,64,256]{3,2,1,0:T(8,128)S(1)} %get-tuple-element.1015), channel_id=1, source_target_pairs={{4,0},{8,4},{12,8},{16,12},{20,16},{24,20},{28,24},{5,1},{9,5},{13... | collective-permute-start | bytes 196616 | tf_op jit(solution)/shard_map/while/body/eval_jaxpr/ppermute | solution.py:21
  246.0 13.1 %collective-permute-start.5 = (f32[1,1,64,256]{3,2,1,0:T(8,128)S(1)}, f32[1,1,64,256]{3,2,1,0:T(8,128)S(1)}, u32[]{:S(2)}, u32[]{:S(2)}) collective-permute-start(f32[1,1,64,256]{3,2,1,0:T(8,128)S(1)} %get-tuple-element.1016), channel_id=1, source_target_pairs={{0,4},{4,8},{8,12},{12,16},{16,20},{20,24},{24,28},{1,5},{5,9},{9,... | collective-permute-start | bytes 196616 | tf_op jit(solution)/shard_map/while/body/eval_jaxpr/ppermute | solution.py:20
  261.0 13.8 %collective-permute-start.4 = (f32[1,1,64,256]{3,2,1,0:T(8,128)S(1)}, f32[1,1,64,256]{3,2,1,0:T(8,128)S(1)}, u32[]{:S(2)}, u32[]{:S(2)}) collective-permute-start(f32[1,1,64,256]{3,2,1,0:T(8,128)S(1)} %get-tuple-element.1015), channel_id=1, source_target_pairs={{4,0},{8,4},{12,8},{16,12},{20,16},{24,20},{28,24},{5,1},{9,5},{13... | collective-permute-start | bytes 196616 | tf_op jit(solution)/shard_map/while/body/eval_jaxpr/ppermute | solution.py:21
  262.3 12.5 %collective-permute-start.5 = (f32[1,1,64,256]{3,2,1,0:T(8,128)S(1)}, f32[1,1,64,256]{3,2,1,0:T(8,128)S(1)}, u32[]{:S(2)}, u32[]{:S(2)}) collective-permute-start(f32[1,1,64,256]{3,2,1,0:T(8,128)S(1)} %get-tuple-element.1016), channel_id=1, source_target_pairs={{0,4},{4,8},{8,12},{12,16},{16,20},{20,24},{24,28},{1,5},{5,9},{9,... | collective-permute-start | bytes 196616 | tf_op jit(solution)/shard_map/while/body/eval_jaxpr/ppermute | solution.py:20
  276.6 13.8 %collective-permute-start.4 = (f32[1,1,64,256]{3,2,1,0:T(8,128)S(1)}, f32[1,1,64,256]{3,2,1,0:T(8,128)S(1)}, u32[]{:S(2)}, u32[]{:S(2)}) collective-permute-start(f32[1,1,64,256]{3,2,1,0:T(8,128)S(1)} %get-tuple-element.1015), channel_id=1, source_target_pairs={{4,0},{8,4},{12,8},{16,12},{20,16},{24,20},{28,24},{5,1},{9,5},{13... | collective-permute-start | bytes 196616 | tf_op jit(solution)/shard_map/while/body/eval_jaxpr/ppermute | solution.py:21
  277.9 12.5 %collective-permute-start.5 = (f32[1,1,64,256]{3,2,1,0:T(8,128)S(1)}, f32[1,1,64,256]{3,2,1,0:T(8,128)S(1)}, u32[]{:S(2)}, u32[]{:S(2)}) collective-permute-start(f32[1,1,64,256]{3,2,1,0:T(8,128)S(1)} %get-tuple-element.1016), channel_id=1, source_target_pairs={{0,4},{4,8},{8,12},{12,16},{16,20},{20,24},{24,28},{1,5},{5,9},{9,... | collective-permute-start | bytes 196616 | tf_op jit(solution)/shard_map/while/body/eval_jaxpr/ppermute | solution.py:20
  292.3 13.9 %collective-permute-start.4 = (f32[1,1,64,256]{3,2,1,0:T(8,128)S(1)}, f32[1,1,64,256]{3,2,1,0:T(8,128)S(1)}, u32[]{:S(2)}, u32[]{:S(2)}) collective-permute-start(f32[1,1,64,256]{3,2,1,0:T(8,128)S(1)} %get-tuple-element.1015), channel_id=1, source_target_pairs={{4,0},{8,4},{12,8},{16,12},{20,16},{24,20},{28,24},{5,1},{9,5},{13... | collective-permute-start | bytes 196616 | tf_op jit(solution)/shard_map/while/body/eval_jaxpr/ppermute | solution.py:21
  293.6 12.6 %collective-permute-start.5 = (f32[1,1,64,256]{3,2,1,0:T(8,128)S(1)}, f32[1,1,64,256]{3,2,1,0:T(8,128)S(1)}, u32[]{:S(2)}, u32[]{:S(2)}) collective-permute-start(f32[1,1,64,256]{3,2,1,0:T(8,128)S(1)} %get-tuple-element.1016), channel_id=1, source_target_pairs={{0,4},{4,8},{8,12},{12,16},{16,20},{20,24},{24,28},{1,5},{5,9},{9,... | collective-permute-start | bytes 196616 | tf_op jit(solution)/shard_map/while/body/eval_jaxpr/ppermute | solution.py:20
  308.1 13.8 %collective-permute-start.4 = (f32[1,1,64,256]{3,2,1,0:T(8,128)S(1)}, f32[1,1,64,256]{3,2,1,0:T(8,128)S(1)}, u32[]{:S(2)}, u32[]{:S(2)}) collective-permute-start(f32[1,1,64,256]{3,2,1,0:T(8,128)S(1)} %get-tuple-element.1015), channel_id=1, source_target_pairs={{4,0},{8,4},{12,8},{16,12},{20,16},{24,20},{28,24},{5,1},{9,5},{13... | collective-permute-start | bytes 196616 | tf_op jit(solution)/shard_map/while/body/eval_jaxpr/ppermute | solution.py:21
  309.4 12.5 %collective-permute-start.5 = (f32[1,1,64,256]{3,2,1,0:T(8,128)S(1)}, f32[1,1,64,256]{3,2,1,0:T(8,128)S(1)}, u32[]{:S(2)}, u32[]{:S(2)}) collective-permute-start(f32[1,1,64,256]{3,2,1,0:T(8,128)S(1)} %get-tuple-element.1016), channel_id=1, source_target_pairs={{0,4},{4,8},{8,12},{12,16},{16,20},{20,24},{24,28},{1,5},{5,9},{9,... | collective-permute-start | bytes 196616 | tf_op jit(solution)/shard_map/while/body/eval_jaxpr/ppermute | solution.py:20
  323.8 13.8 %collective-permute-start.4 = (f32[1,1,64,256]{3,2,1,0:T(8,128)S(1)}, f32[1,1,64,256]{3,2,1,0:T(8,128)S(1)}, u32[]{:S(2)}, u32[]{:S(2)}) collective-permute-start(f32[1,1,64,256]{3,2,1,0:T(8,128)S(1)} %get-tuple-element.1015), channel_id=1, source_target_pairs={{4,0},{8,4},{12,8},{16,12},{20,16},{24,20},{28,24},{5,1},{9,5},{13... | collective-permute-start | bytes 196616 | tf_op jit(solution)/shard_map/while/body/eval_jaxpr/ppermute | solution.py:21
  325.1 12.5 %collective-permute-start.5 = (f32[1,1,64,256]{3,2,1,0:T(8,128)S(1)}, f32[1,1,64,256]{3,2,1,0:T(8,128)S(1)}, u32[]{:S(2)}, u32[]{:S(2)}) collective-permute-start(f32[1,1,64,256]{3,2,1,0:T(8,128)S(1)} %get-tuple-element.1016), channel_id=1, source_target_pairs={{0,4},{4,8},{8,12},{12,16},{16,20},{20,24},{24,28},{1,5},{5,9},{9,... | collective-permute-start | bytes 196616 | tf_op jit(solution)/shard_map/while/body/eval_jaxpr/ppermute | solution.py:20
  339.4 13.8 %collective-permute-start.4 = (f32[1,1,64,256]{3,2,1,0:T(8,128)S(1)}, f32[1,1,64,256]{3,2,1,0:T(8,128)S(1)}, u32[]{:S(2)}, u32[]{:S(2)}) collective-permute-start(f32[1,1,64,256]{3,2,1,0:T(8,128)S(1)} %get-tuple-element.1015), channel_id=1, source_target_pairs={{4,0},{8,4},{12,8},{16,12},{20,16},{24,20},{28,24},{5,1},{9,5},{13... | collective-permute-start | bytes 196616 | tf_op jit(solution)/shard_map/while/body/eval_jaxpr/ppermute | solution.py:21
  355.1 13.8 %collective-permute-start.4 = (f32[1,1,64,256]{3,2,1,0:T(8,128)S(1)}, f32[1,1,64,256]{3,2,1,0:T(8,128)S(1)}, u32[]{:S(2)}, u32[]{:S(2)}) collective-permute-start(f32[1,1,64,256]{3,2,1,0:T(8,128)S(1)} %get-tuple-element.1015), channel_id=1, source_target_pairs={{4,0},{8,4},{12,8},{16,12},{20,16},{24,20},{28,24},{5,1},{9,5},{13... | collective-permute-start | bytes 196616 | tf_op jit(solution)/shard_map/while/body/eval_jaxpr/ppermute | solution.py:21
  370.8 13.8 %collective-permute-start.4 = (f32[1,1,64,256]{3,2,1,0:T(8,128)S(1)}, f32[1,1,64,256]{3,2,1,0:T(8,128)S(1)}, u32[]{:S(2)}, u32[]{:S(2)}) collective-permute-start(f32[1,1,64,256]{3,2,1,0:T(8,128)S(1)} %get-tuple-element.1015), channel_id=1, source_target_pairs={{4,0},{8,4},{12,8},{16,12},{20,16},{24,20},{28,24},{5,1},{9,5},{13... | collective-permute-start | bytes 196616 | tf_op jit(solution)/shard_map/while/body/eval_jaxpr/ppermute | solution.py:21
  386.5 14.0 %collective-permute-start.4 = (f32[1,1,64,256]{3,2,1,0:T(8,128)S(1)}, f32[1,1,64,256]{3,2,1,0:T(8,128)S(1)}, u32[]{:S(2)}, u32[]{:S(2)}) collective-permute-start(f32[1,1,64,256]{3,2,1,0:T(8,128)S(1)} %get-tuple-element.1015), channel_id=1, source_target_pairs={{4,0},{8,4},{12,8},{16,12},{20,16},{24,20},{28,24},{5,1},{9,5},{13... | collective-permute-start | bytes 196616 | tf_op jit(solution)/shard_map/while/body/eval_jaxpr/ppermute | solution.py:21
  387.8 12.7 %collective-permute-start.5 = (f32[1,1,64,256]{3,2,1,0:T(8,128)S(1)}, f32[1,1,64,256]{3,2,1,0:T(8,128)S(1)}, u32[]{:S(2)}, u32[]{:S(2)}) collective-permute-start(f32[1,1,64,256]{3,2,1,0:T(8,128)S(1)} %get-tuple-element.1016), channel_id=1, source_target_pairs={{0,4},{4,8},{8,12},{12,16},{16,20},{20,24},{24,28},{1,5},{5,9},{9,... | collective-permute-start | bytes 196616 | tf_op jit(solution)/shard_map/while/body/eval_jaxpr/ppermute | solution.py:20
  402.4 13.8 %collective-permute-start.4 = (f32[1,1,64,256]{3,2,1,0:T(8,128)S(1)}, f32[1,1,64,256]{3,2,1,0:T(8,128)S(1)}, u32[]{:S(2)}, u32[]{:S(2)}) collective-permute-start(f32[1,1,64,256]{3,2,1,0:T(8,128)S(1)} %get-tuple-element.1015), channel_id=1, source_target_pairs={{4,0},{8,4},{12,8},{16,12},{20,16},{24,20},{28,24},{5,1},{9,5},{13... | collective-permute-start | bytes 196616 | tf_op jit(solution)/shard_map/while/body/eval_jaxpr/ppermute | solution.py:21
  418.1 13.8 %collective-permute-start.4 = (f32[1,1,64,256]{3,2,1,0:T(8,128)S(1)}, f32[1,1,64,256]{3,2,1,0:T(8,128)S(1)}, u32[]{:S(2)}, u32[]{:S(2)}) collective-permute-start(f32[1,1,64,256]{3,2,1,0:T(8,128)S(1)} %get-tuple-element.1015), channel_id=1, source_target_pairs={{4,0},{8,4},{12,8},{16,12},{20,16},{24,20},{28,24},{5,1},{9,5},{13... | collective-permute-start | bytes 196616 | tf_op jit(solution)/shard_map/while/body/eval_jaxpr/ppermute | solution.py:21
  419.4 12.5 %collective-permute-start.5 = (f32[1,1,64,256]{3,2,1,0:T(8,128)S(1)}, f32[1,1,64,256]{3,2,1,0:T(8,128)S(1)}, u32[]{:S(2)}, u32[]{:S(2)}) collective-permute-start(f32[1,1,64,256]{3,2,1,0:T(8,128)S(1)} %get-tuple-element.1016), channel_id=1, source_target_pairs={{0,4},{4,8},{8,12},{12,16},{16,20},{20,24},{24,28},{1,5},{5,9},{9,... | collective-permute-start | bytes 196616 | tf_op jit(solution)/shard_map/while/body/eval_jaxpr/ppermute | solution.py:20
  433.8 13.8 %collective-permute-start.4 = (f32[1,1,64,256]{3,2,1,0:T(8,128)S(1)}, f32[1,1,64,256]{3,2,1,0:T(8,128)S(1)}, u32[]{:S(2)}, u32[]{:S(2)}) collective-permute-start(f32[1,1,64,256]{3,2,1,0:T(8,128)S(1)} %get-tuple-element.1015), channel_id=1, source_target_pairs={{4,0},{8,4},{12,8},{16,12},{20,16},{24,20},{28,24},{5,1},{9,5},{13... | collective-permute-start | bytes 196616 | tf_op jit(solution)/shard_map/while/body/eval_jaxpr/ppermute | solution.py:21
  449.4 13.8 %collective-permute-start.4 = (f32[1,1,64,256]{3,2,1,0:T(8,128)S(1)}, f32[1,1,64,256]{3,2,1,0:T(8,128)S(1)}, u32[]{:S(2)}, u32[]{:S(2)}) collective-permute-start(f32[1,1,64,256]{3,2,1,0:T(8,128)S(1)} %get-tuple-element.1015), channel_id=1, source_target_pairs={{4,0},{8,4},{12,8},{16,12},{20,16},{24,20},{28,24},{5,1},{9,5},{13... | collective-permute-start | bytes 196616 | tf_op jit(solution)/shard_map/while/body/eval_jaxpr/ppermute | solution.py:21
  465.1 13.8 %collective-permute-start.4 = (f32[1,1,64,256]{3,2,1,0:T(8,128)S(1)}, f32[1,1,64,256]{3,2,1,0:T(8,128)S(1)}, u32[]{:S(2)}, u32[]{:S(2)}) collective-permute-start(f32[1,1,64,256]{3,2,1,0:T(8,128)S(1)} %get-tuple-element.1015), channel_id=1, source_target_pairs={{4,0},{8,4},{12,8},{16,12},{20,16},{24,20},{28,24},{5,1},{9,5},{13... | collective-permute-start | bytes 196616 | tf_op jit(solution)/shard_map/while/body/eval_jaxpr/ppermute | solution.py:21
  482.4 81.4 %all-to-all-start = ((f32[4,8,64,256]{3,2,1,0:T(8,128)}), f32[4,8,64,256]{3,2,1,0:T(8,128)S(1)}, u32[]{:S(2)}, u32[]{:S(2)}) async-start(f32[4,8,64,256]{3,2,1,0:T(8,128)} %broadcast_in_dim.80), calls=%async_computation | async-start | bytes 4194304 | tf_op jit(solution)/shard_map/all_to_all | solution.py:34
  (163 other events, 1840.2 us)
where the time goes:
time: 935 us; the launch traced here: 923 us
  starting transfers between devices  518 us (55%)
  waiting for transfers between devices  146 us (16%)
  blocking collectives  108 us (12%)
  other arithmetic  106 us (11%)
  local copies, waits for them, and re-layouts  32 us (3%)
    ppermute x90, starting transfers between devices, with_halo(): lax.ppermute(last, axis, up)  347 us
    ppermute x90, waiting for transfers between devices, with_halo(): lax.ppermute(first, axis, [(b, a) for a, b in up])  119 us
    ppermute x90, starting transfers between devices, with_halo(): lax.ppermute(first, axis, [(b, a) for a, b in up])  116 us
    psum x10, blocking collectives, over_axes(): array = lax.psum(array, axis)  108 us
    all_to_all x1, starting transfers between devices, copy_for_each(): return lax.all_to_all(copies, axis, split_axis=0, concat_axis=0, tiled=True)  55.1 us
    dynamic_update_slice x15, other arithmetic, advance(): history = lax.dynamic_update_index_in_dim(history, advanced, index + 1, 0)  29.9 us
    reduce_sum x15, other arithmetic, propagate(): sampled = jnp.sum(receivers * advanced, axis=3) * live_now[:, None, None]  26.4 us
    all_to_all x1, waiting for transfers between devices, copy_for_each(): return lax.all_to_all(copies, axis, split_axis=0, concat_axis=0, tiled=True)  26.2 us
  transfers between devices with their start and end apart: 181, of which 68 were waited for; matrix products, arithmetic and copies ran while one was open for 2% of the time, Pallas kernels for 0%

commit v1 on v0

v1 whole, which is shorter than its diff:
```python
import functools

import jax
import jax.numpy as jnp
from jax import lax
from jax.experimental import pallas as pl
from jax.experimental.pallas import tpu as pltpu
from jax.sharding import PartitionSpec as P

MESH = pl.DeviceIdType.MESH
F32 = jnp.float32
WAYS = [(-1, 0), (1, 0), (0, -1), (0, 1), (-1, -1), (-1, 1), (1, -1), (1, 1)]
DEEP = 2
TILE = 8


def kernel(
    sizes,
    groups,
    now_h,
    prev_h,
    csq_h,
    refl_h,
    dirn_h,
    oldg_h,
    rec_h,
    source,
    wavelet,
    live,
    image_h,
    dirout_h,
    resid_h,
    misfit_o,
    back,
    adj,
    csq,
    dirn,
    grad,
    gain,
    spot,
    crec,
    recs,
    recv_mask,
    traces,
    oldg,
    refl,
    half_a,
    half_b,
    half_c,
    slots_a,
    slots_b,
    slots_c,
    local_sem,
    start_send,
    start_recv,
    halo_send,
    halo_recv,
    pair_send,
    pair_recv,
    sum_send,
    sum_recv,
    out_sem,
):
    nx, ny, nz, steps, entries = sizes
    shots, gxs, gys = groups
    ex, ey = nx + 2 * DEEP, ny + 2 * TILE
    x_lo, x_hi = DEEP, DEEP + nx
    y_lo, y_hi = TILE, TILE + ny
    shot, gx, gy = lax.axis_index("shot"), lax.axis_index("gx"), lax.axis_index("gy")
    core = lax.rem(shot, 2)

    def has(way):
        at_x, at_y = gx + way[0], gy + way[1]
        return (at_x >= 0) & (at_x < gxs) & (at_y >= 0) & (at_y < gys)

    def regions(way, width):
        dx, dy = way
        src_x, dst_x = {
            -1: ((x_lo, width), (x_hi, width)),
            1: ((x_hi - width, width), (x_lo - width, width)),
            0: ((x_lo, nx), (x_lo, nx)),
        }[dx]
        src_y, dst_y = {
            -1: ((y_lo, TILE), (y_hi, TILE)),
            1: ((y_hi - TILE, TILE), (0, TILE)),
            0: ((y_lo, ny), (y_lo, ny)),
        }[dy]
        return (
            (pl.ds(*src_x), pl.ds(*src_y), slice(None)),
            (pl.ds(*dst_x), pl.ds(*dst_y), slice(None)),
        )

    def halo_copy(ref, k, width, send, recv):
        src, dst = regions(WAYS[k], width)
        return pltpu.make_async_remote_copy(
            src_ref=ref.at[src],
            dst_ref=ref.at[dst],
            send_sem=send.at[k],
            recv_sem=recv.at[k],
            device_id={"gx": gx + WAYS[k][0], "gy": gy + WAYS[k][1]},
            device_id_type=MESH,
        )

    def start_way(ref, k, width, send, recv):
        @pl.when(has(WAYS[k]))
        def _():
            halo_copy(ref, k, width, send, recv).start()

    def start_halo(ref, width, send, recv):
        for k in range(8):
            start_way(ref, k, width, send, recv)

    def wait_halo(ref, width, send, recv):
        for k, way in enumerate(WAYS):
            came = has((-way[0], -way[1]))

            @pl.when(came)
            def _():
                halo_copy(ref, k, width, send, recv).wait_recv()

            @pl.when(jnp.logical_not(came))
            def _():
                where = regions(way, width)[1]
                view = ref.at[where]
                view[...] = jnp.zeros(view.shape, F32)

            @pl.when(has(way))
            def _():
                halo_copy(ref, k, width, send, recv).wait_send()

    inner = (pl.ds(x_lo, nx), pl.ds(y_lo, ny), slice(None))
    loads = [
        (rec_h, traces.at[inner]),
        (csq_h, csq.at[inner]),
        (now_h, back.at[(1,) + inner]),
        (prev_h, back.at[(0,) + inner]),
        (dirn_h, dirn.at[inner]),
        (oldg_h, oldg),
        (refl_h, refl),
    ]
    copies = [
        pltpu.make_async_copy(src, dst, local_sem.at[i]) for i, (src, dst) in enumerate(loads)
    ]
    for copy in copies:
        copy.start()
    starts = [(traces, DEEP), (csq, DEEP), (back.at[1], DEEP), (back.at[0], 1), (dirn, DEEP)]
    for i in range(4):
        copies[i].wait()
        start_halo(starts[i][0], starts[i][1], start_send.at[i], start_recv.at[i])
    for i in range(4, 7):
        copies[i].wait()

    lane = lax.broadcasted_iota(jnp.int32, (ey, nz), 1)
    lane_t = lax.broadcasted_iota(jnp.int32, (ey, 128), 1)
    row = lax.broadcasted_iota(jnp.int32, (ey, nz), 0)
    first, last = lane == 0, lane == nz - 1
    live_here = live[0]
    yz = (row + (gy * ny - TILE) == source[0, 1]) & (lane == source[0, 2])

    @pl.loop(0, ex)
    def _(i):
        adj[0, i] = jnp.zeros((ey, nz), F32)
        hit = yz & (row * 0 + (i + gx * nx - DEEP) == source[0, 0])
        spot[i] = jnp.where(hit, 1.0, 0.0)

    recs[...] = jnp.zeros(recs.shape, F32)
    wait_halo(traces, DEEP, start_send.at[0], start_recv.at[0])
    wait_halo(csq, DEEP, start_send.at[1], start_recv.at[1])

    def column(i, n):
        picked = jnp.where((lane_t == n) & (lane_t < live_here), traces[i], 0.0)
        return jnp.sum(picked, axis=1, keepdims=True)

    @pl.loop(0, ex)
    def _(i):
        depth = jnp.sum(jnp.where(lane_t == steps, traces[i], 0.0), axis=1, keepdims=True)
        here = lane.astype(F32) == depth
        crec[i] = jnp.where(here, csq[i], 0.0)
        adj[1, i] = crec[i] * column(i, steps - 1)

    @pl.loop(0, nx)
    def _(i):
        depth = jnp.sum(
            jnp.where(lane_t == steps, traces[i + x_lo], 0.0), axis=1, keepdims=True
        )
        here = lane.astype(F32) == depth
        recv_mask[i] = jnp.where(here, 1.0, 0.0)[y_lo:y_hi]

    def plane(field, s, i, whole, extra):
        v = field[s, i]
        cut = slice(0, ey) if whole else slice(y_lo, y_hi)
        rows = pl.ds(0, ey) if whole else pl.ds(y_lo, ny)
        mid = v[cut]
        total = field[s, i - 1, rows, :] + field[s, i + 1, rows, :]
        total = total + (pltpu.roll(v, 1, 0) + pltpu.roll(v, ey - 1, 0))[cut]
        left = jnp.where(first[cut], 0.0, pltpu.roll(mid, 1, 1))
        right = jnp.where(last[cut], 0.0, pltpu.roll(mid, nz - 1, 1))
        total = total + left + right
        value = csq[i, rows, :] * (total - 6.0 * mid)
        value = value + (2.0 * mid - field[s - 1, i, rows, :]) + extra(i, rows, cut)
        field[s + 1, i, rows, :] = value

    def planes(field, s, lo, hi, whole, extra):
        @pl.loop(lo, hi)
        def _(i):
            plane(field, s, i, whole, extra)

    def ahead(s):
        amount = wavelet[0, s - 1]
        return lambda i, rows, cut: amount * spot[i, rows, :]

    def behind(s):
        return lambda i, rows, cut: crec[i, rows, :] * column(i, steps - 1 - s)[cut]

    def scattered(s):
        return lambda i, rows, cut: gain[i, rows, :] * back[s + 1, i, rows, :]

    def advance(field, s, make, send, recv):
        planes(field, s, x_lo - 1, x_hi + 1, True, make(s))
        extra = make(s + 1)
        target = field.at[s + 2]
        planes(field, s + 1, x_lo, x_lo + DEEP, False, extra)
        start_way(target, 0, DEEP, send, recv)
        planes(field, s + 1, x_hi - DEEP, x_hi, False, extra)
        start_way(target, 1, DEEP, send, recv)
        for k in range(4, 8):
            start_way(target, k, DEEP, send, recv)
        planes(field, s + 1, x_lo + DEEP, x_hi - DEEP, False, extra)
        start_way(target, 2, DEEP, send, recv)
        start_way(target, 3, DEEP, send, recv)

    blocks = (steps - 1) // 2

    @pl.loop(0, blocks)
    def _(j):
        s = 2 * j + 1
        now, before = lax.rem(j, 2), lax.rem(j + 1, 2)
        for field, way, make in ((adj, 1, behind), (back, 0, ahead)):

            @pl.when(j > 0)
            def _():
                wait_halo(field.at[s], DEEP, halo_send.at[way, before], halo_recv.at[way, before])

            if way == 0:

                @pl.when(j == 0)
                def _():
                    wait_halo(back.at[1], DEEP, start_send.at[2], start_recv.at[2])
                    wait_halo(back.at[0], 1, start_send.at[3], start_recv.at[3])

            advance(field, s, make, halo_send.at[way, now], halo_recv.at[way, now])

    end = 2 * blocks + 1
    final = (blocks - 1) % 2
    for field, way, make in ((adj, 1, behind), (back, 0, ahead)):
        wait_halo(field.at[end], DEEP, halo_send.at[way, final], halo_recv.at[way, final])
        planes(field, end, x_lo, x_hi, False, make(end))

    start_halo(dirn, DEEP, start_send.at[4], start_recv.at[4])

    half = nx // 2
    partner = {"shot": shot + 1 - 2 * core}
    opposite = {"shot": lax.rem(shot + 2, shots)}
    mine, other = x_lo + half * core, x_lo + half * (1 - core)
    own_half = (pl.ds(mine, half), pl.ds(y_lo, ny), slice(None))

    def products(start, keep):
        @pl.loop(start, start + half)
        def _(i):
            total = back[1, i, y_lo:y_hi, :] * adj[steps, i, y_lo:y_hi, :]
            for a in range(2, steps + 1):
                total = total + back[a, i, y_lo:y_hi, :] * adj[steps + 1 - a, i, y_lo:y_hi, :]
            keep(i, total)

    def pair_copy(src, dst, k, device):
        return pltpu.make_async_remote_copy(
            src_ref=src,
            dst_ref=dst,
            send_sem=pair_send.at[k],
            recv_sem=pair_recv.at[k],
            device_id=device,
            device_id_type=MESH,
        )

    def keep_other(i, total):
        half_c[i - other] = total

    def keep_mine(i, total):
        grad[i, y_lo:y_hi, :] = total

    products(other, keep_other)
    swap_a = pair_copy(half_c, half_a, 0, partner)
    swap_a.start()
    products(mine, keep_mine)
    swap_a.wait()

    def add_half(buffer):
        @pl.loop(0, half)
        def _(i):
            grad[mine + i, y_lo:y_hi, :] = grad[mine + i, y_lo:y_hi, :] + buffer[i]

    add_half(half_a)
    swap_b = pair_copy(grad.at[own_half], half_b, 1, opposite)
    swap_b.start()
    swap_b.wait()
    add_half(half_b)
    spread = pair_copy(grad.at[own_half], grad.at[own_half], 2, partner)
    spread.start()

    def fold(values):
        return jnp.sum(values.reshape(-1, 8, 128), axis=0)

    def lanes(values):
        return values[:, :128] + values[:, 128:]

    def dots(i, sums):
        g = grad[mine + i, y_lo:y_hi, :]
        o = oldg[mine + i - x_lo]
        d = dirn[mine + i, y_lo:y_hi, :]
        parts = [fold(lanes(a * b)) for a, b in ((g, g), (g, o), (o, o), (g, d))]
        return tuple(s + p for s, p in zip(sums, parts))

    zero = jnp.zeros((8, 128), F32)
    sums = lax.fori_loop(0, half, dots, (zero,) * 4)
    gy_core = gys * 2
    place = gy * 2 + core

    def gx_member(k):
        return {"gx": k}

    def side_member(k):
        return {"gy": k // 2, "shot": shot - core + lax.rem(k, 2)}

    def all_sum(values, slots, at, count, member, base):
        slots[at] = values

        def copy(peer, slot):
            return pltpu.make_async_remote_copy(
                src_ref=slots.at[at],
                dst_ref=slots.at[slot],
                send_sem=sum_send.at[base, peer],
                recv_sem=sum_recv.at[base, slot],
                device_id=member(peer),
                device_id_type=MESH,
            )

        for o in range(1, count):
            copy(lax.rem(at + o, count), at).start()
        for o in range(1, count):
            source_at = lax.rem(at + count - o, count)
            copy(source_at, source_at).wait_recv()
        for o in range(1, count):
            copy(lax.rem(at + o, count), at).wait_send()
        total = slots[0]
        for k in range(1, count):
            total = total + slots[k]
        return total

    def reduce_all(values):
        return jnp.sum(jnp.sum(values, axis=1, keepdims=True), axis=0, keepdims=True)

    stacked = jnp.stack(sums)
    spread.wait_recv()
    start_halo(grad, DEEP, start_send.at[0], start_recv.at[0])
    stacked = all_sum(stacked, slots_a.at[0], gx, gxs, gx_member, 0)
    stacked = all_sum(stacked, slots_b.at[0], place, gy_core, side_member, 1)
    grad_sq, cross, old_sq, toward = [reduce_all(stacked[k]) for k in range(4)]
    beta = (grad_sq - cross) / old_sq
    slope = grad_sq + beta * toward
    spread.wait_send()
    wait_halo(dirn, DEEP, start_send.at[4], start_recv.at[4])
    wait_halo(grad, DEEP, start_send.at[0], start_recv.at[0])

    @pl.loop(0, ex)
    def _(i):
        onward = grad[i] + beta * dirn[i]
        dirn[i] = onward
        gain[i] = csq[i] * onward
        adj[1, i] = gain[i] * back[1, i]

    def sample(s):
        @pl.loop(0, nx)
        def _(i):
            seen = adj[s, i + x_lo, y_lo:y_hi, :] * recv_mask[i]
            value = jnp.sum(seen, axis=1, keepdims=True)
            recs[i] = jnp.where(lane_t[:ny] == s - 1, value, recs[i])

    out_dir = pltpu.make_async_copy(dirn.at[inner], dirout_h, out_sem.at[0])
    sample(1)
    out_dir.start()

    @pl.loop(0, blocks)
    def _(j):
        s = 2 * j + 1
        now, before = lax.rem(j, 2), lax.rem(j + 1, 2)

        @pl.when(j > 0)
        def _():
            wait_halo(adj.at[s], DEEP, halo_send.at[2, before], halo_recv.at[2, before])

        advance(adj, s, scattered, halo_send.at[2, now], halo_recv.at[2, now])
        sample(s + 1)
        sample(s + 2)

    wait_halo(adj.at[end], DEEP, halo_send.at[2, final], halo_recv.at[2, final])
    planes(adj, end, x_lo, x_hi, False, scattered(end))
    sample(end + 1)

    lane_r = lane_t[:ny]
    told = lane_r < live_here
    kept = lane_r < steps

    def score(i, sums):
        rec = jnp.where(told, recs[i], 0.0)
        res = jnp.where(kept, traces[i + x_lo, y_lo:y_hi, :], 0.0)
        recs[i] = rec
        parts = [fold(a * b) for a, b in ((rec, rec), (rec, res), (res, res))]
        return tuple(s + p for s, p in zip(sums, parts))

    sums = lax.fori_loop(0, nx, score, (zero,) * 3)
    stacked = jnp.stack(sums + (zero,))
    stacked = all_sum(stacked, slots_a.at[1], gx, gxs, gx_member, 2)
    stacked = all_sum(stacked, slots_b.at[1], place, gy_core, side_member, 3)
    upper = shot // 2
    stacked = all_sum(
        stacked, slots_c, upper, shots // 2, lambda k: {"shot": k * 2 + core}, 4
    )
    rec_sq, rec_res, res_sq = [reduce_all(stacked[k]) for k in range(3)]
    length = slope / rec_sq

    @pl.loop(0, nx)
    def _(i):
        refl[i] = refl[i] + length * dirn[i + x_lo, y_lo:y_hi, :]

    out_image = pltpu.make_async_copy(refl, image_h, out_sem.at[1])
    out_image.start()

    @pl.loop(0, nx)
    def _(i):
        recs[i] = traces[i + x_lo, y_lo:y_hi, :] - length * recs[i]

    out_resid = pltpu.make_async_copy(recs, resid_h, out_sem.at[2])
    out_resid.start()
    misfit = res_sq - 2.0 * length * rec_res + length * length * rec_sq
    misfit_o[...] = jnp.broadcast_to(misfit * (0.5 / entries), (8, 128))
    out_dir.wait()
    out_image.wait()
    out_resid.wait()


def on_device(groups, *arguments):
    (now, prev, csq, refl, dirn, oldg, residual, depth, source, wavelet, live) = arguments
    now, prev = now[0], prev[0]
    nx, ny, nz = now.shape
    steps = residual.shape[1]
    entries = float(residual.size * groups[0] * groups[1] * groups[2])
    ex, ey = nx + 2 * DEEP, ny + 2 * TILE
    traces = jnp.concatenate([residual[0], depth.astype(F32)], axis=0)
    traces = jnp.pad(jnp.transpose(traces, (1, 2, 0)), ((0, 0), (0, 0), (0, 127 - steps)))
    whole = pl.BlockSpec(memory_space=pl.ANY)
    small = pl.BlockSpec(memory_space=pltpu.SMEM)
    grow = pltpu.VMEM((ex, ey, nz), F32)
    dma = pltpu.SemaphoreType.DMA
    image, onward, resid, misfit = pl.pallas_call(
        functools.partial(kernel, (nx, ny, nz, steps, entries), groups),
        out_shape=(
            jax.ShapeDtypeStruct((nx, ny, nz), F32),
            jax.ShapeDtypeStruct((nx, ny, nz), F32),
            jax.ShapeDtypeStruct((nx, ny, 128), F32),
            jax.ShapeDtypeStruct((8, 128), F32),
        ),
        in_specs=[whole] * 7 + [small] * 3,
        out_specs=(whole, whole, whole, pl.BlockSpec(memory_space=pltpu.VMEM)),
        scratch_shapes=[
            pltpu.VMEM((steps + 1, ex, ey, nz), F32),
            pltpu.VMEM((steps + 1, ex, ey, nz), F32),
            grow,
            grow,
            grow,
            grow,
            grow,
            grow,
            pltpu.VMEM((nx, ny, 128), F32),
            pltpu.VMEM((nx, ny, nz), F32),
            pltpu.VMEM((ex, ey, 128), F32),
            pltpu.VMEM((nx, ny, nz), F32),
            pltpu.VMEM((nx, ny, nz), F32),
            pltpu.VMEM((nx // 2, ny, nz), F32),
            pltpu.VMEM((nx // 2, ny, nz), F32),
            pltpu.VMEM((nx // 2, ny, nz), F32),
            pltpu.VMEM((2, groups[1], 4, 8, 128), F32),
            pltpu.VMEM((2, groups[2] * 2, 4, 8, 128), F32),
            pltpu.VMEM((groups[0] // 2, 4, 8, 128), F32),
            dma((7,)),
            dma((5, 8)),
            dma((5, 8)),
            dma((3, 2, 8)),
            dma((3, 2, 8)),
            dma((3,)),
            dma((3,)),
            dma((5, 8)),
            dma((5, 8)),
            dma((3,)),
        ],
        compiler_params=pltpu.CompilerParams(
            has_side_effects=True, vmem_limit_bytes=62 * 1024 * 1024
        ),
        name="iteration",
    )(now, prev, csq, refl, dirn, oldg, traces, source, wavelet, live)
    resid = jnp.transpose(resid[:, :, :steps], (2, 0, 1))[None]
    return image, onward, resid, misfit[0, 0]


def solution(mesh):
    groups = (mesh.shape["shot"], mesh.shape["gx"], mesh.shape["gy"])
    space = P("gx", "gy", None)
    placed = (
        P("shot", "gx", "gy", None),
        P("shot", "gx", "gy", None),
        space,
        space,
        space,
        space,
        P("shot", None, "gx", "gy"),
        P("shot", "gx", "gy"),
        P("shot", None),
        P("shot", None),
        P("shot"),
    )
    return jax.shard_map(
        functools.partial(on_device, groups),
        mesh=mesh,
        in_specs=placed,
        out_specs=(space, space, P("shot", None, "gx", "gy"), P()),
        check_vma=False,
    )
```

time: 935 us -> 188 us (0.20); the launches traced: 923 us -> 188 us
  starting transfers between devices: 518 us -> 0 us
  Pallas kernels: 0 us -> 180 us
  waiting for transfers between devices: 146 us -> 0 us
  blocking collectives: 108 us -> 0 us
  other arithmetic: 106 us -> 0.85 us
  local copies, waits for them, and re-layouts: 32 us -> 5.89 us
    ppermute x180 -> x0, starting transfers between devices: 463 us -> none  [the longest x90 347 us: with_halo(): lax.ppermute(last, axis, up)]
    pallas_call x0 -> x1, Pallas kernels: none -> 180 us  [on_device(): pl.pallas_call(functools.partial(kernel, (nx, ny, nz, steps, entries), gr...]
    ppermute x180 -> x0, waiting for transfers between devices: 120 us -> none  [the longest x90 119 us: with_halo(): lax.ppermute(first, axis, [(b, a) for a, b in up])]
    psum x10 -> x0, blocking collectives: 108 us -> none  [over_axes(): array = lax.psum(array, axis)]
    all_to_all x1 -> x0, starting transfers between devices: 55.1 us -> none  [copy_for_each(): return lax.all_to_all(copies, axis, split_axis=0, concat_axis=0, tiled=True)]
    dynamic_update_slice x30 -> x0, other arithmetic: 39.6 us -> none  [the longest x15 29.9 us: advance(): history = lax.dynamic_update_index_in_dim(history, advanced, index + 1, 0)]
    reduce_sum x19 -> x0, other arithmetic: 31.3 us -> none  [the longest x15 26.4 us: propagate(): sampled = jnp.sum(receivers * advanced, axis=3) * live_now[:, None, None]]
    add x16 -> x0, other arithmetic: 27.4 us -> none  [the longest x15 25.5 us: retreat(): return (current, following, summed + wavefield * current)]
  transfers between devices with their start and end apart: 181 -> 0, of which waited for: 68 -> 0; matrix products, arithmetic and copies ran while one was open for 2% -> 0% of each run, Pallas kernels for 0% -> 0%
where the time goes in v1:
time: 188 us
  Pallas kernels  180 us (96%)
  local copies, waits for them, and re-layouts  5.89 us (3%)
    pallas_call x1, Pallas kernels, on_device(): pl.pallas_call(functools.partial(kernel, (nx, ny, nz, steps, entries), gr...  180 us

profile of v1, /device:TPU:1, one launch (start us, length us, event | category | flops | bytes accessed | tf_op | source)
XLA Modules:
  0.0 188.1 jit_solution(8292928453166413374)
XLA Ops:
  0.6 0.0 copy-start.2
  1.3 0.0 copy-done.2
  1.3 0.8 pad_maximum_fusion
  2.2 0.1 copy.18
  2.3 0.7 pad.4.rec_h
  3.1 180.1 %iteration.1 = (f32[8,64,256]{2,1,0:T(8,128)}, f32[8,64,256]{2,1,0:T(8,128)}, f32[8,64,128]{2,1,0:T(8,128)}, f32[8,128]{1,0:T(8,128)}) custom-call(f32[8,64,256]{2,1,0:T(8,128)} %bitcast.10, f32[8,64,256]{2,1,0:T(8,128)} %bitcast.11, f32[8,64,256]{2,1,0:T(8,128)} %csq_h.1, f32[8,64,256]{2,1,0:T(8,128)} %refl_h.1, f32[8,64,256]{2,1,0:T(8,128)} %dirn_h.1, ...), custom_call_target="tpu_custom_call" | custom-call | tf_op jit(solution)/shard_map/iteration/pallas_call | solution.py:464
  183.1 0.0 copy-start.1
  183.1 1.2 slice.7
  184.4 1.0 slice_bitcast_fusion
  185.3 0.8 copy.19
  186.1 0.0 copy-done.1
  186.1 0.0 copy-start
  186.1 0.8 copy.23
  186.9 0.4 copy-done
  187.3 0.8 copy.24
  (1 shorter events, 0.0 us)
Async XLA Ops:
  0.6 0.7 copy-start.2
  183.1 3.0 %copy-start.1 = (f32[8,64,256]{2,1,0:T(8,128)S(1)}, f32[8,64,256]{2,1,0:T(8,128)}, u32[]{:S(2)}) copy-start(f32[8,64,256]{2,1,0:T(8,128)} %get-tuple-element.24) | copy-start | bytes 1572868
  186.1 1.2 copy-start

commit v2 on v1

--- a/solution.py
+++ b/solution.py
@@ -12,6 +12,7 @@
 WAYS = [(-1, 0), (1, 0), (0, -1), (0, 1), (-1, -1), (-1, 1), (1, -1), (1, 1)]
 DEEP = 2
 TILE = 8
+LANES = 128
 
 
 def kernel(
@@ -39,6 +40,7 @@
     gain,
     spot,
     crec,
+    twice,
     recs,
     recv_mask,
     traces,
@@ -63,6 +65,7 @@
 ):
     nx, ny, nz, steps, entries = sizes
     shots, gxs, gys = groups
+    parts = nz // LANES
     ex, ey = nx + 2 * DEEP, ny + 2 * TILE
     x_lo, x_hi = DEEP, DEEP + nx
     y_lo, y_hi = TILE, TILE + ny
@@ -86,8 +89,8 @@
             0: ((y_lo, ny), (y_lo, ny)),
         }[dy]
         return (
-            (pl.ds(*src_x), pl.ds(*src_y), slice(None)),
-            (pl.ds(*dst_x), pl.ds(*dst_y), slice(None)),
+            (pl.ds(*src_x), slice(None), pl.ds(*src_y), slice(None)),
+            (pl.ds(*dst_x), slice(None), pl.ds(*dst_y), slice(None)),
         )
 
     def halo_copy(ref, k, width, send, recv):
@@ -128,92 +131,132 @@
             def _():
                 halo_copy(ref, k, width, send, recv).wait_send()
 
-    inner = (pl.ds(x_lo, nx), pl.ds(y_lo, ny), slice(None))
+    xs, ys = pl.ds(x_lo, nx), pl.ds(y_lo, ny)
+
+    def halves(array, view):
+        return [
+            (array.at[:, :, pl.ds(h * LANES, LANES)], view.at[:, h]) for h in range(parts)
+        ]
+
+    def inside(ref):
+        return ref.at[xs, :, ys, :]
+
     loads = [
-        (rec_h, traces.at[inner]),
-        (csq_h, csq.at[inner]),
-        (now_h, back.at[(1,) + inner]),
-        (prev_h, back.at[(0,) + inner]),
-        (dirn_h, dirn.at[inner]),
-        (oldg_h, oldg),
-        (refl_h, refl),
+        [(rec_h, traces.at[xs, 0, ys, :])],
+        halves(csq_h, inside(csq)),
+        halves(now_h, inside(back.at[1])),
+        halves(prev_h, inside(back.at[0])),
+        halves(dirn_h, inside(dirn)),
+        halves(oldg_h, oldg),
+        halves(refl_h, refl),
     ]
     copies = [
-        pltpu.make_async_copy(src, dst, local_sem.at[i]) for i, (src, dst) in enumerate(loads)
+        [pltpu.make_async_copy(src, dst, local_sem.at[i, h]) for h, (src, dst) in enumerate(pairs)]
+        for i, pairs in enumerate(loads)
     ]
-    for copy in copies:
-        copy.start()
+    for pairs in copies:
+        for copy in pairs:
+            copy.start()
     starts = [(traces, DEEP), (csq, DEEP), (back.at[1], DEEP), (back.at[0], 1), (dirn, DEEP)]
     for i in range(4):
-        copies[i].wait()
+        for copy in copies[i]:
+            copy.wait()
         start_halo(starts[i][0], starts[i][1], start_send.at[i], start_recv.at[i])
     for i in range(4, 7):
-        copies[i].wait()
-
-    lane = lax.broadcasted_iota(jnp.int32, (ey, nz), 1)
-    lane_t = lax.broadcasted_iota(jnp.int32, (ey, 128), 1)
-    row = lax.broadcasted_iota(jnp.int32, (ey, nz), 0)
-    first, last = lane == 0, lane == nz - 1
+        for copy in copies[i]:
+            copy.wait()
+
+    lane = lax.broadcasted_iota(jnp.int32, (ey, LANES), 1)
+    row = lax.broadcasted_iota(jnp.int32, (ey, LANES), 0)
     live_here = live[0]
-    yz = (row + (gy * ny - TILE) == source[0, 1]) & (lane == source[0, 2])
 
     @pl.loop(0, ex)
     def _(i):
-        adj[0, i] = jnp.zeros((ey, nz), F32)
-        hit = yz & (row * 0 + (i + gx * nx - DEEP) == source[0, 0])
-        spot[i] = jnp.where(hit, 1.0, 0.0)
+        for h in range(parts):
+            adj[0, i, h] = jnp.zeros((ey, LANES), F32)
+            hit = (row + (gy * ny - TILE) == source[0, 1]) & (lane + h * LANES == source[0, 2])
+            hit = hit & (row * 0 + (i + gx * nx - DEEP) == source[0, 0])
+            spot[i, h] = jnp.where(hit, 1.0, 0.0)
 
     recs[...] = jnp.zeros(recs.shape, F32)
     wait_halo(traces, DEEP, start_send.at[0], start_recv.at[0])
     wait_halo(csq, DEEP, start_send.at[1], start_recv.at[1])
 
-    def column(i, n):
-        picked = jnp.where((lane_t == n) & (lane_t < live_here), traces[i], 0.0)
+    def column(i, n, r, count):
+        at = lane[:count]
+        picked = jnp.where((at == n) & (at < live_here), traces[i, 0, r : r + count, :], 0.0)
         return jnp.sum(picked, axis=1, keepdims=True)
+
+    def receivers(i):
+        level = jnp.sum(jnp.where(lane == steps, traces[i, 0], 0.0), axis=1, keepdims=True)
+        return [(lane + h * LANES).astype(F32) == level for h in range(parts)]
 
     @pl.loop(0, ex)
     def _(i):
-        depth = jnp.sum(jnp.where(lane_t == steps, traces[i], 0.0), axis=1, keepdims=True)
-        here = lane.astype(F32) == depth
-        crec[i] = jnp.where(here, csq[i], 0.0)
-        adj[1, i] = crec[i] * column(i, steps - 1)
+        newest = column(i, steps - 1, 0, ey)
+        for h, here in enumerate(receivers(i)):
+            crec[i, h] = jnp.where(here, csq[i, h], 0.0)
+            adj[1, i, h] = crec[i, h] * newest
+            twice[i, h] = 2.0 - 6.0 * csq[i, h]
 
     @pl.loop(0, nx)
     def _(i):
-        depth = jnp.sum(
-            jnp.where(lane_t == steps, traces[i + x_lo], 0.0), axis=1, keepdims=True
-        )
-        here = lane.astype(F32) == depth
-        recv_mask[i] = jnp.where(here, 1.0, 0.0)[y_lo:y_hi]
+        for h, here in enumerate(receivers(i + x_lo)):
+            recv_mask[i, h] = jnp.where(here, 1.0, 0.0)[y_lo:y_hi]
+
+    def strip(field, s, i, r, count, extra):
+        at = lane[:count]
+        first, last = at == 0, at == LANES - 1
+        rows = pl.ds(r, count)
+        mids = [field[s, i, h, rows, :] for h in range(parts)]
+        ups = [pltpu.roll(mid, 1, 1) for mid in mids]
+        downs = [pltpu.roll(mid, LANES - 1, 1) for mid in mids]
+        for h, mid in enumerate(mids):
+            before = ups[h - 1] if h > 0 else 0.0
+            after = downs[h + 1] if h < parts - 1 else 0.0
+            left = jnp.where(first, before, ups[h])
+            right = jnp.where(last, after, downs[h])
+            if r > 0:
+                above = field[s, i, h, pl.ds(r - 1, count), :]
+            else:
+                above = pltpu.roll(mid, 1, 0)
+            if r + count < ey:
+                below = field[s, i, h, pl.ds(r + 1, count), :]
+            else:
+                below = pltpu.roll(mid, count - 1, 0)
+            total = (field[s, i - 1, h, rows, :] + field[s, i + 1, h, rows, :]) + (above + below)
+            total = total + (left + right)
+            value = csq[i, h, rows, :] * total + twice[i, h, rows, :] * mid
+            value = value - field[s - 1, i, h, rows, :] + extra(i, h, r, count)
+            field[s + 1, i, h, rows, :] = value
 
     def plane(field, s, i, whole, extra):
-        v = field[s, i]
-        cut = slice(0, ey) if whole else slice(y_lo, y_hi)
-        rows = pl.ds(0, ey) if whole else pl.ds(y_lo, ny)
-        mid = v[cut]
-        total = field[s, i - 1, rows, :] + field[s, i + 1, rows, :]
-        total = total + (pltpu.roll(v, 1, 0) + pltpu.roll(v, ey - 1, 0))[cut]
-        left = jnp.where(first[cut], 0.0, pltpu.roll(mid, 1, 1))
-        right = jnp.where(last[cut], 0.0, pltpu.roll(mid, nz - 1, 1))
-        total = total + left + right
-        value = csq[i, rows, :] * (total - 6.0 * mid)
-        value = value + (2.0 * mid - field[s - 1, i, rows, :]) + extra(i, rows, cut)
-        field[s + 1, i, rows, :] = value
+        if whole:
+            strip(field, s, i, 0, TILE, extra(i, 0, TILE))
+        strip(field, s, i, y_lo, ny, extra(i, y_lo, ny))
+        if whole:
+            strip(field, s, i, y_hi, TILE, extra(i, y_hi, TILE))
 
     def planes(field, s, lo, hi, whole, extra):
-        @pl.loop(lo, hi)
+        @pl.loop(lo, hi, unroll=2)
         def _(i):
             plane(field, s, i, whole, extra)
 
     def ahead(s):
         amount = wavelet[0, s - 1]
-        return lambda i, rows, cut: amount * spot[i, rows, :]
+        return lambda *_: lambda i, h, r, count: amount * spot[i, h, r : r + count, :]
 
     def behind(s):
-        return lambda i, rows, cut: crec[i, rows, :] * column(i, steps - 1 - s)[cut]
+        def at_plane(i, r, count):
+            weight = column(i, steps - 1 - s, r, count)
+            return lambda i, h, r, count: crec[i, h, r : r + count, :] * weight
+
+        return at_plane
 
     def scattered(s):
-        return lambda i, rows, cut: gain[i, rows, :] * back[s + 1, i, rows, :]
+        return lambda *_: (
+            lambda i, h, r, count: gain[i, h, r : r + count, :] * back[s + 1, i, h, r : r + count, :]
+        )
 
     def advance(field, s, make, send, recv):
         planes(field, s, x_lo - 1, x_hi + 1, True, make(s))
@@ -262,15 +305,17 @@
     partner = {"shot": shot + 1 - 2 * core}
     opposite = {"shot": lax.rem(shot + 2, shots)}
     mine, other = x_lo + half * core, x_lo + half * (1 - core)
-    own_half = (pl.ds(mine, half), pl.ds(y_lo, ny), slice(None))
+    own_half = (pl.ds(mine, half), slice(None), ys, slice(None))
 
     def products(start, keep):
         @pl.loop(start, start + half)
         def _(i):
-            total = back[1, i, y_lo:y_hi, :] * adj[steps, i, y_lo:y_hi, :]
-            for a in range(2, steps + 1):
-                total = total + back[a, i, y_lo:y_hi, :] * adj[steps + 1 - a, i, y_lo:y_hi, :]
-            keep(i, total)
+            for h in range(parts):
+                total = back[1, i, h, y_lo:y_hi, :] * adj[steps, i, h, y_lo:y_hi, :]
+                for a in range(2, steps + 1):
+                    one, two = back[a, i, h, y_lo:y_hi, :], adj[steps + 1 - a, i, h, y_lo:y_hi, :]
+                    total = total + one * two
+                keep(i, h, total)
 
     def pair_copy(src, dst, k, device):
         return pltpu.make_async_remote_copy(
@@ -282,11 +327,11 @@
             device_id_type=MESH,
         )
 
-    def keep_other(i, total):
-        half_c[i - other] = total
-
-    def keep_mine(i, total):
-        grad[i, y_lo:y_hi, :] = total
+    def keep_other(i, h, total):
+        half_c[i - other, h] = total
+
+    def keep_mine(i, h, total):
+        grad[i, h, y_lo:y_hi, :] = total
 
     products(other, keep_other)
     swap_a = pair_copy(half_c, half_a, 0, partner)
@@ -297,7 +342,9 @@
     def add_half(buffer):
         @pl.loop(0, half)
         def _(i):
-            grad[mine + i, y_lo:y_hi, :] = grad[mine + i, y_lo:y_hi, :] + buffer[i]
+            for h in range(parts):
+                was = grad[mine + i, h, y_lo:y_hi, :]
+                grad[mine + i, h, y_lo:y_hi, :] = was + buffer[i, h]
 
     add_half(half_a)
     swap_b = pair_copy(grad.at[own_half], half_b, 1, opposite)
@@ -308,19 +355,29 @@
     spread.start()
 
     def fold(values):
-        return jnp.sum(values.reshape(-1, 8, 128), axis=0)
-
-    def lanes(values):
-        return values[:, :128] + values[:, 128:]
+        return jnp.sum(values.reshape(-1, 8, LANES), axis=0)
 
     def dots(i, sums):
-        g = grad[mine + i, y_lo:y_hi, :]
-        o = oldg[mine + i - x_lo]
-        d = dirn[mine + i, y_lo:y_hi, :]
-        parts = [fold(lanes(a * b)) for a, b in ((g, g), (g, o), (o, o), (g, d))]
-        return tuple(s + p for s, p in zip(sums, parts))
-
-    zero = jnp.zeros((8, 128), F32)
+        for h in range(parts):
+            g = grad[mine + i, h, y_lo:y_hi, :]
+            o = oldg[mine + i - x_lo, h]
+            d = dirn[mine + i, h, y_lo:y_hi, :]
+            added = [fold(a * b) for a, b in ((g, g), (g, o), (o, o), (g, d))]
+            sums = tuple(s + p for s, p in zip(sums, added))
+        return sums
+
+    zero = jnp.zeros((8, LANES), F32)
+    eight = lax.broadcasted_iota(jnp.int32, (8, LANES), 0)
+
+    def pack(sums):
+        packed = zero
+        for k, value in enumerate(sums):
+            packed = jnp.where(eight == k, jnp.sum(value, axis=0, keepdims=True), packed)
+        return packed
+
+    def unpack(packed, k):
+        return jnp.sum(packed[k : k + 1], axis=1, keepdims=True)
+
     sums = lax.fori_loop(0, half, dots, (zero,) * 4)
     gy_core = gys * 2
     place = gy * 2 + core
@@ -356,15 +413,12 @@
             total = total + slots[k]
         return total
 
-    def reduce_all(values):
-        return jnp.sum(jnp.sum(values, axis=1, keepdims=True), axis=0, keepdims=True)
-
-    stacked = jnp.stack(sums)
+    stacked = pack(sums)
     spread.wait_recv()
     start_halo(grad, DEEP, start_send.at[0], start_recv.at[0])
     stacked = all_sum(stacked, slots_a.at[0], gx, gxs, gx_member, 0)
     stacked = all_sum(stacked, slots_b.at[0], place, gy_core, side_member, 1)
-    grad_sq, cross, old_sq, toward = [reduce_all(stacked[k]) for k in range(4)]
+    grad_sq, cross, old_sq, toward = [unpack(stacked, k) for k in range(4)]
     beta = (grad_sq - cross) / old_sq
     slope = grad_sq + beta * toward
     spread.wait_send()
@@ -373,21 +427,28 @@
 
     @pl.loop(0, ex)
     def _(i):
-        onward = grad[i] + beta * dirn[i]
-        dirn[i] = onward
-        gain[i] = csq[i] * onward
-        adj[1, i] = gain[i] * back[1, i]
+        for h in range(parts):
+            onward = grad[i, h] + beta * dirn[i, h]
+            dirn[i, h] = onward
+            gain[i, h] = csq[i, h] * onward
+            adj[1, i, h] = gain[i, h] * back[1, i, h]
 
     def sample(s):
-        @pl.loop(0, nx)
+        @pl.loop(0, nx, unroll=2)
         def _(i):
-            seen = adj[s, i + x_lo, y_lo:y_hi, :] * recv_mask[i]
+            seen = adj[s, i + x_lo, 0, y_lo:y_hi, :] * recv_mask[i, 0]
+            for h in range(1, parts):
+                seen = seen + adj[s, i + x_lo, h, y_lo:y_hi, :] * recv_mask[i, h]
             value = jnp.sum(seen, axis=1, keepdims=True)
-            recs[i] = jnp.where(lane_t[:ny] == s - 1, value, recs[i])
-
-    out_dir = pltpu.make_async_copy(dirn.at[inner], dirout_h, out_sem.at[0])
+            recs[i] = jnp.where(lane[:ny] == s - 1, value, recs[i])
+
+    out_dir = [
+        pltpu.make_async_copy(src, dst, out_sem.at[0, h])
+        for h, (dst, src) in enumerate(halves(dirout_h, inside(dirn)))
+    ]
     sample(1)
-    out_dir.start()
+    for copy in out_dir:
+        copy.start()
 
     @pl.loop(0, blocks)
     def _(j):
@@ -406,45 +467,50 @@
     planes(adj, end, x_lo, x_hi, False, scattered(end))
     sample(end + 1)
 
-    lane_r = lane_t[:ny]
+    lane_r = lane[:ny]
     told = lane_r < live_here
     kept = lane_r < steps
 
     def score(i, sums):
         rec = jnp.where(told, recs[i], 0.0)
-        res = jnp.where(kept, traces[i + x_lo, y_lo:y_hi, :], 0.0)
+        res = jnp.where(kept, traces[i + x_lo, 0, y_lo:y_hi, :], 0.0)
         recs[i] = rec
-        parts = [fold(a * b) for a, b in ((rec, rec), (rec, res), (res, res))]
-        return tuple(s + p for s, p in zip(sums, parts))
+        added = [fold(a * b) for a, b in ((rec, rec), (rec, res), (res, res))]
+        return tuple(s + p for s, p in zip(sums, added))
 
     sums = lax.fori_loop(0, nx, score, (zero,) * 3)
-    stacked = jnp.stack(sums + (zero,))
+    stacked = pack(sums)
     stacked = all_sum(stacked, slots_a.at[1], gx, gxs, gx_member, 2)
     stacked = all_sum(stacked, slots_b.at[1], place, gy_core, side_member, 3)
     upper = shot // 2
     stacked = all_sum(
         stacked, slots_c, upper, shots // 2, lambda k: {"shot": k * 2 + core}, 4
     )
-    rec_sq, rec_res, res_sq = [reduce_all(stacked[k]) for k in range(3)]
+    rec_sq, rec_res, res_sq = [unpack(stacked, k) for k in range(3)]
     length = slope / rec_sq
 
     @pl.loop(0, nx)
     def _(i):
-        refl[i] = refl[i] + length * dirn[i + x_lo, y_lo:y_hi, :]
-
-    out_image = pltpu.make_async_copy(refl, image_h, out_sem.at[1])
-    out_image.start()
+        for h in range(parts):
+            refl[i, h] = refl[i, h] + length * dirn[i + x_lo, h, y_lo:y_hi, :]
+
+    out_image = [
+        pltpu.make_async_copy(src, dst, out_sem.at[1, h])
+        for h, (dst, src) in enumerate(halves(image_h, refl))
+    ]
+    for copy in out_image:
+        copy.start()
 
     @pl.loop(0, nx)
     def _(i):
-        recs[i] = traces[i + x_lo, y_lo:y_hi, :] - length * recs[i]
-
-    out_resid = pltpu.make_async_copy(recs, resid_h, out_sem.at[2])
+        recs[i] = traces[i + x_lo, 0, y_lo:y_hi, :] - length * recs[i]
+
+    out_resid = pltpu.make_async_copy(recs, resid_h, out_sem.at[2, 0])
     out_resid.start()
     misfit = res_sq - 2.0 * length * rec_res + length * length * rec_sq
     misfit_o[...] = jnp.broadcast_to(misfit * (0.5 / entries), (8, 128))
-    out_dir.wait()
-    out_image.wait()
+    for copy in out_dir + out_image:
+        copy.wait()
     out_resid.wait()
 
 
@@ -459,7 +525,11 @@
     traces = jnp.pad(jnp.transpose(traces, (1, 2, 0)), ((0, 0), (0, 0), (0, 127 - steps)))
     whole = pl.BlockSpec(memory_space=pl.ANY)
     small = pl.BlockSpec(memory_space=pltpu.SMEM)
-    grow = pltpu.VMEM((ex, ey, nz), F32)
+    parts = nz // LANES
+    grow = pltpu.VMEM((ex, parts, ey, LANES), F32)
+    block = pltpu.VMEM((nx, parts, ny, LANES), F32)
+    piece = pltpu.VMEM((nx // 2, parts, ny, LANES), F32)
+    history = pltpu.VMEM((steps + 1, ex, parts, ey, LANES), F32)
     dma = pltpu.SemaphoreType.DMA
     image, onward, resid, misfit = pl.pallas_call(
         functools.partial(kernel, (nx, ny, nz, steps, entries), groups),
@@ -472,26 +542,27 @@
         in_specs=[whole] * 7 + [small] * 3,
         out_specs=(whole, whole, whole, pl.BlockSpec(memory_space=pltpu.VMEM)),
         scratch_shapes=[
-            pltpu.VMEM((steps + 1, ex, ey, nz), F32),
-            pltpu.VMEM((steps + 1, ex, ey, nz), F32),
+            history,
+            history,
             grow,
             grow,
             grow,
             grow,
             grow,
             grow,
-            pltpu.VMEM((nx, ny, 128), F32),
-            pltpu.VMEM((nx, ny, nz), F32),
-            pltpu.VMEM((ex, ey, 128), F32),
-            pltpu.VMEM((nx, ny, nz), F32),
-            pltpu.VMEM((nx, ny, nz), F32),
-            pltpu.VMEM((nx // 2, ny, nz), F32),
-            pltpu.VMEM((nx // 2, ny, nz), F32),
-            pltpu.VMEM((nx // 2, ny, nz), F32),
-            pltpu.VMEM((2, groups[1], 4, 8, 128), F32),
-            pltpu.VMEM((2, groups[2] * 2, 4, 8, 128), F32),
-            pltpu.VMEM((groups[0] // 2, 4, 8, 128), F32),
-            dma((7,)),
+            grow,
+            pltpu.VMEM((nx, ny, LANES), F32),
+            block,
+            pltpu.VMEM((ex, 1, ey, LANES), F32),
+            block,
+            block,
+            piece,
+            piece,
+            piece,
+            pltpu.VMEM((2, groups[1], 8, LANES), F32),
+            pltpu.VMEM((2, groups[2] * 2, 8, LANES), F32),
+            pltpu.VMEM((groups[0] // 2, 8, LANES), F32),
+            dma((7, parts)),
             dma((5, 8)),
             dma((5, 8)),
             dma((3, 2, 8)),
@@ -500,7 +571,7 @@
             dma((3,)),
             dma((5, 8)),
             dma((5, 8)),
-            dma((3,)),
+            dma((3, parts)),
         ],
         compiler_params=pltpu.CompilerParams(
             has_side_effects=True, vmem_limit_bytes=62 * 1024 * 1024

time: 188 us -> 181 us (0.963)
  Pallas kernels: 180 us -> 173 us
    pallas_call x1, Pallas kernels: 180 us -> 173 us  [on_device(): pl.pallas_call(functools.partial(kernel, (nx, ny, nz, steps, entries), gr...]
where the time goes in v2:
time: 181 us
  Pallas kernels  173 us (96%)
  local copies, waits for them, and re-layouts  5.89 us (3%)
    pallas_call x1, Pallas kernels, on_device(): pl.pallas_call(functools.partial(kernel, (nx, ny, nz, steps, entries), gr...  173 us

profile of v2, /device:TPU:1, one launch (start us, length us, event | category | flops | bytes accessed | tf_op | source)
XLA Modules:
  0.0 181.1 jit_solution(12734662704682442417)
XLA Ops:
  0.6 0.0 copy-start.2
  1.3 0.0 copy-done.2
  1.3 0.8 pad_maximum_fusion
  2.2 0.1 copy.18
  2.3 0.7 pad.4.rec_h
  3.1 173.0 %iteration.1 = (f32[8,64,256]{2,1,0:T(8,128)}, f32[8,64,256]{2,1,0:T(8,128)}, f32[8,64,128]{2,1,0:T(8,128)}, f32[8,128]{1,0:T(8,128)}) custom-call(f32[8,64,256]{2,1,0:T(8,128)} %bitcast.10, f32[8,64,256]{2,1,0:T(8,128)} %bitcast.11, f32[8,64,256]{2,1,0:T(8,128)} %csq_h.1, f32[8,64,256]{2,1,0:T(8,128)} %refl_h.1, f32[8,64,256]{2,1,0:T(8,128)} %dirn_h.1, ...), custom_call_target="tpu_custom_call" | custom-call | tf_op jit(solution)/shard_map/iteration/pallas_call | solution.py:534
  176.1 0.0 copy-start.1
  176.1 1.2 slice.7
  177.3 1.0 slice_bitcast_fusion
  178.3 0.8 copy.19
  179.0 0.0 copy-done.1
  179.0 0.0 copy-start
  179.0 0.8 copy.23
  179.8 0.4 copy-done
  180.3 0.8 copy.24
  (1 shorter events, 0.0 us)
Async XLA Ops:
  0.6 0.7 copy-start.2
  176.1 3.0 %copy-start.1 = (f32[8,64,256]{2,1,0:T(8,128)S(1)}, f32[8,64,256]{2,1,0:T(8,128)}, u32[]{:S(2)}) copy-start(f32[8,64,256]{2,1,0:T(8,128)} %get-tuple-element.24) | copy-start | bytes 1572868
  179.0 1.2 copy-start

commit v3 on v2

--- a/solution.py
+++ b/solution.py
@@ -24,7 +24,8 @@
     refl_h,
     dirn_h,
     oldg_h,
-    rec_h,
+    res_h,
+    depth_h,
     source,
     wavelet,
     live,
@@ -44,8 +45,16 @@
     recs,
     recv_mask,
     traces,
+    weights,
+    csq_s,
+    now_s,
+    prev_s,
+    dirn_s,
     oldg,
     refl,
+    res_s,
+    depth_s,
+    resid_s,
     half_a,
     half_b,
     half_c,
@@ -133,38 +142,52 @@
 
     xs, ys = pl.ds(x_lo, nx), pl.ds(y_lo, ny)
 
-    def halves(array, view):
-        return [
-            (array.at[:, :, pl.ds(h * LANES, LANES)], view.at[:, h]) for h in range(parts)
-        ]
-
-    def inside(ref):
-        return ref.at[xs, :, ys, :]
-
     loads = [
-        [(rec_h, traces.at[xs, 0, ys, :])],
-        halves(csq_h, inside(csq)),
-        halves(now_h, inside(back.at[1])),
-        halves(prev_h, inside(back.at[0])),
-        halves(dirn_h, inside(dirn)),
-        halves(oldg_h, oldg),
-        halves(refl_h, refl),
+        (res_h, res_s),
+        (depth_h, depth_s),
+        (csq_h, csq_s),
+        (now_h, now_s),
+        (prev_h, prev_s),
+        (dirn_h, dirn_s),
+        (oldg_h, oldg),
+        (refl_h, refl),
     ]
     copies = [
-        [pltpu.make_async_copy(src, dst, local_sem.at[i, h]) for h, (src, dst) in enumerate(pairs)]
-        for i, pairs in enumerate(loads)
+        pltpu.make_async_copy(src, dst, local_sem.at[i]) for i, (src, dst) in enumerate(loads)
     ]
-    for pairs in copies:
-        for copy in pairs:
-            copy.start()
-    starts = [(traces, DEEP), (csq, DEEP), (back.at[1], DEEP), (back.at[0], 1), (dirn, DEEP)]
-    for i in range(4):
-        for copy in copies[i]:
-            copy.wait()
-        start_halo(starts[i][0], starts[i][1], start_send.at[i], start_recv.at[i])
-    for i in range(4, 7):
-        for copy in copies[i]:
-            copy.wait()
+    for copy in copies:
+        copy.start()
+
+    half = nx // 2
+    gy_core = gys * 2
+    place = gy * 2 + core
+    partner = {"shot": shot + 1 - 2 * core}
+    opposite = {"shot": lax.rem(shot + 2, shots)}
+
+    def gx_member(k):
+        return {"gx": k}
+
+    def side_member(k):
+        return {"gy": k // 2, "shot": shot - core + lax.rem(k, 2)}
+
+    barrier = pltpu.get_barrier_semaphore()
+
+    def greet(device):
+        pl.semaphore_signal(barrier, inc=1, device_id=device, device_id_type=MESH)
+
+    for o in range(1, gxs):
+        greet(gx_member(lax.rem(gx + o, gxs)))
+    for o in range(1, gy_core):
+        greet(side_member(lax.rem(place + o, gy_core)))
+    greet(opposite)
+    met = jnp.int32(gxs + gy_core - 1)
+    for way in WAYS[4:]:
+
+        @pl.when(has(way))
+        def _():
+            greet({"gx": gx + way[0], "gy": gy + way[1]})
+
+        met = met + has(way).astype(jnp.int32)
 
     lane = lax.broadcasted_iota(jnp.int32, (ey, LANES), 1)
     row = lax.broadcasted_iota(jnp.int32, (ey, LANES), 0)
@@ -179,8 +202,43 @@
             spot[i, h] = jnp.where(hit, 1.0, 0.0)
 
     recs[...] = jnp.zeros(recs.shape, F32)
+
+    def unpack_rows(source_ref, target):
+        for i in range(nx):
+            for h in range(parts):
+                target[i + x_lo, h, y_lo:y_hi, :] = source_ref[i, :, h * LANES : (h + 1) * LANES]
+
+    starts = [(traces, DEEP), (csq, DEEP), (back.at[1], DEEP), (back.at[0], 1), (dirn, DEEP)]
+
+    def start_first(i):
+        start_halo(starts[i][0], starts[i][1], start_send.at[i], start_recv.at[i])
+
+    copies[0].wait()
+    copies[1].wait()
+    depths = depth_s[...].astype(F32)
+    top = lax.broadcasted_iota(jnp.int32, (8, ny), 0)
+    for i in range(nx):
+        level = jnp.where(top == 0, depths[i : i + 1], 0.0)
+        rest = jnp.zeros((LANES - steps - 8, ny), F32)
+        stack = jnp.concatenate([res_s[:, i, :], level, rest], axis=0)
+        traces[i + x_lo, 0, y_lo:y_hi, :] = jnp.transpose(stack)
+    pl.semaphore_wait(barrier, met)
+    start_first(0)
+    copies[2].wait()
+    unpack_rows(csq_s, csq.at[...])
+    start_first(1)
+    copies[3].wait()
+    unpack_rows(now_s, back.at[1])
+    start_first(2)
+    copies[4].wait()
+    unpack_rows(prev_s, back.at[0])
+    start_first(3)
+    copies[5].wait()
+    unpack_rows(dirn_s, dirn.at[...])
+    copies[6].wait()
+    copies[7].wait()
+
     wait_halo(traces, DEEP, start_send.at[0], start_recv.at[0])
-    wait_halo(csq, DEEP, start_send.at[1], start_recv.at[1])
 
     def column(i, n, r, count):
         at = lane[:count]
@@ -193,10 +251,16 @@
 
     @pl.loop(0, ex)
     def _(i):
-        newest = column(i, steps - 1, 0, ey)
+        for n in range(steps):
+            weights[n, i] = jnp.broadcast_to(column(i, n, 0, ey), (ey, LANES))
+
+    wait_halo(csq, DEEP, start_send.at[1], start_recv.at[1])
+
+    @pl.loop(0, ex)
+    def _(i):
         for h, here in enumerate(receivers(i)):
             crec[i, h] = jnp.where(here, csq[i, h], 0.0)
-            adj[1, i, h] = crec[i, h] * newest
+            adj[1, i, h] = crec[i, h] * weights[steps - 1, i]
             twice[i, h] = 2.0 - 6.0 * csq[i, h]
 
     @pl.loop(0, nx)
@@ -232,10 +296,10 @@
 
     def plane(field, s, i, whole, extra):
         if whole:
-            strip(field, s, i, 0, TILE, extra(i, 0, TILE))
-        strip(field, s, i, y_lo, ny, extra(i, y_lo, ny))
+            strip(field, s, i, 0, TILE, extra)
+        strip(field, s, i, y_lo, ny, extra)
         if whole:
-            strip(field, s, i, y_hi, TILE, extra(i, y_hi, TILE))
+            strip(field, s, i, y_hi, TILE, extra)
 
     def planes(field, s, lo, hi, whole, extra):
         @pl.loop(lo, hi, unroll=2)
@@ -244,31 +308,30 @@
 
     def ahead(s):
         amount = wavelet[0, s - 1]
-        return lambda *_: lambda i, h, r, count: amount * spot[i, h, r : r + count, :]
+        return lambda i, h, r, count: amount * spot[i, h, r : r + count, :]
 
     def behind(s):
-        def at_plane(i, r, count):
-            weight = column(i, steps - 1 - s, r, count)
-            return lambda i, h, r, count: crec[i, h, r : r + count, :] * weight
-
-        return at_plane
+        n = steps - 1 - s
+        return lambda i, h, r, count: crec[i, h, r : r + count, :] * weights[n, i, r : r + count, :]
 
     def scattered(s):
-        return lambda *_: (
-            lambda i, h, r, count: gain[i, h, r : r + count, :] * back[s + 1, i, h, r : r + count, :]
+        return lambda i, h, r, count: (
+            gain[i, h, r : r + count, :] * back[s + 1, i, h, r : r + count, :]
         )
 
     def advance(field, s, make, send, recv):
-        planes(field, s, x_lo - 1, x_hi + 1, True, make(s))
-        extra = make(s + 1)
+        first, second = make(s), make(s + 1)
         target = field.at[s + 2]
-        planes(field, s + 1, x_lo, x_lo + DEEP, False, extra)
+        planes(field, s, x_lo - 1, x_lo + DEEP + 1, True, first)
+        planes(field, s + 1, x_lo, x_lo + DEEP, False, second)
         start_way(target, 0, DEEP, send, recv)
-        planes(field, s + 1, x_hi - DEEP, x_hi, False, extra)
+        planes(field, s, x_hi - DEEP - 1, x_hi + 1, True, first)
+        planes(field, s + 1, x_hi - DEEP, x_hi, False, second)
         start_way(target, 1, DEEP, send, recv)
         for k in range(4, 8):
             start_way(target, k, DEEP, send, recv)
-        planes(field, s + 1, x_lo + DEEP, x_hi - DEEP, False, extra)
+        planes(field, s, x_lo + DEEP + 1, x_hi - DEEP - 1, True, first)
+        planes(field, s + 1, x_lo + DEEP, x_hi - DEEP, False, second)
         start_way(target, 2, DEEP, send, recv)
         start_way(target, 3, DEEP, send, recv)
 
@@ -299,11 +362,8 @@
         wait_halo(field.at[end], DEEP, halo_send.at[way, final], halo_recv.at[way, final])
         planes(field, end, x_lo, x_hi, False, make(end))
 
-    start_halo(dirn, DEEP, start_send.at[4], start_recv.at[4])
-
-    half = nx // 2
-    partner = {"shot": shot + 1 - 2 * core}
-    opposite = {"shot": lax.rem(shot + 2, shots)}
+    start_first(4)
+
     mine, other = x_lo + half * core, x_lo + half * (1 - core)
     own_half = (pl.ds(mine, half), slice(None), ys, slice(None))
 
@@ -360,7 +420,7 @@
     def dots(i, sums):
         for h in range(parts):
             g = grad[mine + i, h, y_lo:y_hi, :]
-            o = oldg[mine + i - x_lo, h]
+            o = oldg[mine + i - x_lo, :, h * LANES : (h + 1) * LANES]
             d = dirn[mine + i, h, y_lo:y_hi, :]
             added = [fold(a * b) for a, b in ((g, g), (g, o), (o, o), (g, d))]
             sums = tuple(s + p for s, p in zip(sums, added))
@@ -379,15 +439,6 @@
         return jnp.sum(packed[k : k + 1], axis=1, keepdims=True)
 
     sums = lax.fori_loop(0, half, dots, (zero,) * 4)
-    gy_core = gys * 2
-    place = gy * 2 + core
-
-    def gx_member(k):
-        return {"gx": k}
-
-    def side_member(k):
-        return {"gy": k // 2, "shot": shot - core + lax.rem(k, 2)}
-
     def all_sum(values, slots, at, count, member, base):
         slots[at] = values
 
@@ -442,13 +493,14 @@
             value = jnp.sum(seen, axis=1, keepdims=True)
             recs[i] = jnp.where(lane[:ny] == s - 1, value, recs[i])
 
-    out_dir = [
-        pltpu.make_async_copy(src, dst, out_sem.at[0, h])
-        for h, (dst, src) in enumerate(halves(dirout_h, inside(dirn)))
-    ]
+    @pl.loop(0, nx)
+    def _(i):
+        for h in range(parts):
+            dirn_s[i, :, h * LANES : (h + 1) * LANES] = dirn[i + x_lo, h, y_lo:y_hi, :]
+
+    out_dir = pltpu.make_async_copy(dirn_s, dirout_h, out_sem.at[0])
+    out_dir.start()
     sample(1)
-    for copy in out_dir:
-        copy.start()
 
     @pl.loop(0, blocks)
     def _(j):
@@ -492,25 +544,21 @@
     @pl.loop(0, nx)
     def _(i):
         for h in range(parts):
-            refl[i, h] = refl[i, h] + length * dirn[i + x_lo, h, y_lo:y_hi, :]
-
-    out_image = [
-        pltpu.make_async_copy(src, dst, out_sem.at[1, h])
-        for h, (dst, src) in enumerate(halves(image_h, refl))
-    ]
-    for copy in out_image:
-        copy.start()
-
-    @pl.loop(0, nx)
-    def _(i):
-        recs[i] = traces[i + x_lo, 0, y_lo:y_hi, :] - length * recs[i]
-
-    out_resid = pltpu.make_async_copy(recs, resid_h, out_sem.at[2, 0])
+            span = slice(h * LANES, (h + 1) * LANES)
+            refl[i, :, span] = refl[i, :, span] + length * dirn[i + x_lo, h, y_lo:y_hi, :]
+
+    out_image = pltpu.make_async_copy(refl, image_h, out_sem.at[1])
+    out_image.start()
+    for i in range(nx):
+        rest = traces[i + x_lo, 0, y_lo:y_hi, :] - length * recs[i]
+        resid_s[:, i, :] = jnp.transpose(rest)[:steps]
+
+    out_resid = pltpu.make_async_copy(resid_s, resid_h, out_sem.at[2])
     out_resid.start()
     misfit = res_sq - 2.0 * length * rec_res + length * length * rec_sq
     misfit_o[...] = jnp.broadcast_to(misfit * (0.5 / entries), (8, 128))
-    for copy in out_dir + out_image:
-        copy.wait()
+    out_dir.wait()
+    out_image.wait()
     out_resid.wait()
 
 
@@ -521,13 +569,12 @@
     steps = residual.shape[1]
     entries = float(residual.size * groups[0] * groups[1] * groups[2])
     ex, ey = nx + 2 * DEEP, ny + 2 * TILE
-    traces = jnp.concatenate([residual[0], depth.astype(F32)], axis=0)
-    traces = jnp.pad(jnp.transpose(traces, (1, 2, 0)), ((0, 0), (0, 0), (0, 127 - steps)))
     whole = pl.BlockSpec(memory_space=pl.ANY)
     small = pl.BlockSpec(memory_space=pltpu.SMEM)
     parts = nz // LANES
     grow = pltpu.VMEM((ex, parts, ey, LANES), F32)
     block = pltpu.VMEM((nx, parts, ny, LANES), F32)
+    stage = pltpu.VMEM((nx, ny, nz), F32)
     piece = pltpu.VMEM((nx // 2, parts, ny, LANES), F32)
     history = pltpu.VMEM((steps + 1, ex, parts, ey, LANES), F32)
     dma = pltpu.SemaphoreType.DMA
@@ -536,10 +583,10 @@
         out_shape=(
             jax.ShapeDtypeStruct((nx, ny, nz), F32),
             jax.ShapeDtypeStruct((nx, ny, nz), F32),
-            jax.ShapeDtypeStruct((nx, ny, 128), F32),
+            jax.ShapeDtypeStruct((steps, nx, ny), F32),
             jax.ShapeDtypeStruct((8, 128), F32),
         ),
-        in_specs=[whole] * 7 + [small] * 3,
+        in_specs=[whole] * 8 + [small] * 3,
         out_specs=(whole, whole, whole, pl.BlockSpec(memory_space=pltpu.VMEM)),
         scratch_shapes=[
             history,
@@ -554,15 +601,23 @@
             pltpu.VMEM((nx, ny, LANES), F32),
             block,
             pltpu.VMEM((ex, 1, ey, LANES), F32),
-            block,
-            block,
+            pltpu.VMEM((steps, ex, ey, LANES), F32),
+            stage,
+            stage,
+            stage,
+            stage,
+            stage,
+            stage,
+            pltpu.VMEM((steps, nx, ny), F32),
+            pltpu.VMEM((nx, ny), jnp.int32),
+            pltpu.VMEM((steps, nx, ny), F32),
             piece,
             piece,
             piece,
             pltpu.VMEM((2, groups[1], 8, LANES), F32),
             pltpu.VMEM((2, groups[2] * 2, 8, LANES), F32),
             pltpu.VMEM((groups[0] // 2, 8, LANES), F32),
-            dma((7, parts)),
+            dma((8,)),
             dma((5, 8)),
             dma((5, 8)),
             dma((3, 2, 8)),
@@ -571,15 +626,14 @@
             dma((3,)),
             dma((5, 8)),
             dma((5, 8)),
-            dma((3, parts)),
+            dma((3,)),
         ],
         compiler_params=pltpu.CompilerParams(
-            has_side_effects=True, vmem_limit_bytes=62 * 1024 * 1024
+            has_side_effects=True, collective_id=0, vmem_limit_bytes=62 * 1024 * 1024
         ),
         name="iteration",
-    )(now, prev, csq, refl, dirn, oldg, traces, source, wavelet, live)
-    resid = jnp.transpose(resid[:, :, :steps], (2, 0, 1))[None]
-    return image, onward, resid, misfit[0, 0]
+    )(now, prev, csq, refl, dirn, oldg, residual[0], depth[0], source, wavelet, live)
+    return image, onward, resid[None], misfit[0, 0]
 
 
 def solution(mesh):

time: 181 us -> 166 us (0.917)
  Pallas kernels: 173 us -> 159 us
    pallas_call x1, Pallas kernels: 173 us -> 159 us  [on_device(): pl.pallas_call(functools.partial(kernel, (nx, ny, nz, steps, entries), gr...]
where the time goes in v3:
time: 166 us; the launch traced here: 165 us
  Pallas kernels  159 us (96%)
  local copies, waits for them, and re-layouts  4.61 us (3%)
    pallas_call x1, Pallas kernels, on_device(): pl.pallas_call(functools.partial(kernel, (nx, ny, nz, steps, entries), gr...  159 us
    unnamed x7, local copies, waits for them, and re-layouts  3.42 us

profile of v3, /device:TPU:1, one launch (start us, length us, event | category | flops | bytes accessed | tf_op | source)
XLA Modules:
  0.0 165.3 jit_solution(3492771893890911743)
XLA Ops:
  1.3 159.4 %iteration.1 = (f32[8,64,256]{2,1,0:T(8,128)}, f32[8,64,256]{2,1,0:T(8,128)}, f32[16,8,64]{2,1,0:T(8,128)}, f32[8,128]{1,0:T(8,128)}) custom-call(f32[8,64,256]{2,1,0:T(8,128)} %bitcast.6, f32[8,64,256]{2,1,0:T(8,128)} %bitcast.7, f32[8,64,256]{2,1,0:T(8,128)} %csq_h.1, f32[8,64,256]{2,1,0:T(8,128)} %refl_h.1, f32[8,64,256]{2,1,0:T(8,128)} %dirn_h.1, ...), custom_call_target="tpu_custom_call" | custom-call | tf_op jit(solution)/shard_map/iteration/pallas_call | solution.py:581
  160.7 1.2 slice.3
  161.9 0.0 copy-start
  161.9 1.9 %copy.19 = f32[8,64,256]{2,1,0:T(8,128)} copy(f32[8,64,256]{2,1,0:T(8,128)} %get-tuple-element.16) | data formatting | bytes 1048576
  163.8 0.0 copy-done
  163.8 0.0 copy-start.1
  163.8 0.8 copy.20
  164.6 0.1 copy-done.1
  164.7 0.6 copy.21
Async XLA Ops:
  161.9 1.9 %copy-start = (f32[8,64,256]{2,1,0:T(8,128)S(1)}, f32[8,64,256]{2,1,0:T(8,128)}, u32[]{:S(2)}) copy-start(f32[8,64,256]{2,1,0:T(8,128)} %get-tuple-element.17) | copy-start | bytes 1572868
  163.8 0.9 copy-start.1

commit v4 on v3

--- a/solution.py
+++ b/solution.py
@@ -21,7 +21,6 @@
     now_h,
     prev_h,
     csq_h,
-    refl_h,
     dirn_h,
     oldg_h,
     res_h,
@@ -29,10 +28,9 @@
     source,
     wavelet,
     live,
-    image_h,
-    dirout_h,
-    resid_h,
-    misfit_o,
+    grad_h,
+    born_h,
+    scalars_o,
     back,
     adj,
     csq,
@@ -51,7 +49,6 @@
     prev_s,
     dirn_s,
     oldg,
-    refl,
     res_s,
     depth_s,
     resid_s,
@@ -119,7 +116,7 @@
             halo_copy(ref, k, width, send, recv).start()
 
     def start_halo(ref, width, send, recv):
-        for k in range(8):
+        for k in (4, 5, 6, 7, 0, 1, 2, 3):
             start_way(ref, k, width, send, recv)
 
     def wait_halo(ref, width, send, recv):
@@ -150,7 +147,6 @@
         (prev_h, prev_s),
         (dirn_h, dirn_s),
         (oldg_h, oldg),
-        (refl_h, refl),
     ]
     copies = [
         pltpu.make_async_copy(src, dst, local_sem.at[i]) for i, (src, dst) in enumerate(loads)
@@ -170,6 +166,11 @@
     def side_member(k):
         return {"gy": k // 2, "shot": shot - core + lax.rem(k, 2)}
 
+    wide = gy * shots + shot
+
+    def wide_member(k):
+        return {"gy": k // shots, "shot": lax.rem(k, shots)}
+
     barrier = pltpu.get_barrier_semaphore()
 
     def greet(device):
@@ -177,10 +178,9 @@
 
     for o in range(1, gxs):
         greet(gx_member(lax.rem(gx + o, gxs)))
-    for o in range(1, gy_core):
-        greet(side_member(lax.rem(place + o, gy_core)))
-    greet(opposite)
-    met = jnp.int32(gxs + gy_core - 1)
+    for o in range(1, gys * shots):
+        greet(wide_member(lax.rem(wide + o, gys * shots)))
+    met = jnp.int32(gxs + gys * shots - 2)
     for way in WAYS[4:]:
 
         @pl.when(has(way))
@@ -236,7 +236,6 @@
     copies[5].wait()
     unpack_rows(dirn_s, dirn.at[...])
     copies[6].wait()
-    copies[7].wait()
 
     wait_halo(traces, DEEP, start_send.at[0], start_recv.at[0])
 
@@ -324,11 +323,11 @@
         target = field.at[s + 2]
         planes(field, s, x_lo - 1, x_lo + DEEP + 1, True, first)
         planes(field, s + 1, x_lo, x_lo + DEEP, False, second)
-        start_way(target, 0, DEEP, send, recv)
+        for k in (4, 5, 0):
+            start_way(target, k, DEEP, send, recv)
         planes(field, s, x_hi - DEEP - 1, x_hi + 1, True, first)
         planes(field, s + 1, x_hi - DEEP, x_hi, False, second)
-        start_way(target, 1, DEEP, send, recv)
-        for k in range(4, 8):
+        for k in (6, 7, 1):
             start_way(target, k, DEEP, send, recv)
         planes(field, s, x_lo + DEEP + 1, x_hi - DEEP - 1, True, first)
         planes(field, s + 1, x_lo + DEEP, x_hi - DEEP, False, second)
@@ -365,54 +364,59 @@
     start_first(4)
 
     mine, other = x_lo + half * core, x_lo + half * (1 - core)
-    own_half = (pl.ds(mine, half), slice(None), ys, slice(None))
-
-    def products(start, keep):
-        @pl.loop(start, start + half)
-        def _(i):
-            for h in range(parts):
-                total = back[1, i, h, y_lo:y_hi, :] * adj[steps, i, h, y_lo:y_hi, :]
-                for a in range(2, steps + 1):
-                    one, two = back[a, i, h, y_lo:y_hi, :], adj[steps + 1 - a, i, h, y_lo:y_hi, :]
-                    total = total + one * two
-                keep(i, h, total)
-
-    def pair_copy(src, dst, k, device):
+
+    def product(i, h):
+        total = back[1, i, h, y_lo:y_hi, :] * adj[steps, i, h, y_lo:y_hi, :]
+        for a in range(2, steps + 1):
+            one, two = back[a, i, h, y_lo:y_hi, :], adj[steps + 1 - a, i, h, y_lo:y_hi, :]
+            total = total + one * two
+        return total
+
+    def pair_copy(src, dst, k, p, device):
         return pltpu.make_async_remote_copy(
             src_ref=src,
             dst_ref=dst,
-            send_sem=pair_send.at[k],
-            recv_sem=pair_recv.at[k],
+            send_sem=pair_send.at[k, p],
+            recv_sem=pair_recv.at[k, p],
             device_id=device,
             device_id_type=MESH,
         )
 
-    def keep_other(i, h, total):
-        half_c[i - other, h] = total
-
-    def keep_mine(i, h, total):
-        grad[i, h, y_lo:y_hi, :] = total
-
-    products(other, keep_other)
-    swap_a = pair_copy(half_c, half_a, 0, partner)
-    swap_a.start()
-    products(mine, keep_mine)
-    swap_a.wait()
-
-    def add_half(buffer):
-        @pl.loop(0, half)
-        def _(i):
-            for h in range(parts):
-                was = grad[mine + i, h, y_lo:y_hi, :]
-                grad[mine + i, h, y_lo:y_hi, :] = was + buffer[i, h]
-
-    add_half(half_a)
-    swap_b = pair_copy(grad.at[own_half], half_b, 1, opposite)
-    swap_b.start()
-    swap_b.wait()
-    add_half(half_b)
-    spread = pair_copy(grad.at[own_half], grad.at[own_half], 2, partner)
-    spread.start()
+    def own_plane(p):
+        return grad.at[mine + p, :, ys, :]
+
+    def swap_a(p):
+        return pair_copy(half_c.at[p], half_a.at[p], 0, p, partner)
+
+    def swap_b(p):
+        return pair_copy(own_plane(p), half_b.at[p], 1, p, opposite)
+
+    def spread(p):
+        return pair_copy(own_plane(p), own_plane(p), 2, p, partner)
+
+    def add_plane(p, buffer):
+        for h in range(parts):
+            grad[mine + p, h, y_lo:y_hi, :] = grad[mine + p, h, y_lo:y_hi, :] + buffer[p, h]
+
+    @pl.loop(0, half)
+    def _(p):
+        for h in range(parts):
+            half_c[p, h] = product(other + p, h)
+        swap_a(p).start()
+
+    @pl.loop(0, half)
+    def _(p):
+        for h in range(parts):
+            grad[mine + p, h, y_lo:y_hi, :] = product(mine + p, h)
+        swap_a(p).wait()
+        add_plane(p, half_a)
+        swap_b(p).start()
+
+    @pl.loop(0, half)
+    def _(p):
+        swap_b(p).wait()
+        add_plane(p, half_b)
+        spread(p).start()
 
     def fold(values):
         return jnp.sum(values.reshape(-1, 8, LANES), axis=0)
@@ -465,14 +469,16 @@
         return total
 
     stacked = pack(sums)
-    spread.wait_recv()
+    for p in range(half):
+        spread(p).wait_recv()
     start_halo(grad, DEEP, start_send.at[0], start_recv.at[0])
     stacked = all_sum(stacked, slots_a.at[0], gx, gxs, gx_member, 0)
-    stacked = all_sum(stacked, slots_b.at[0], place, gy_core, side_member, 1)
+    stacked = all_sum(stacked, slots_b, place, gy_core, side_member, 1)
     grad_sq, cross, old_sq, toward = [unpack(stacked, k) for k in range(4)]
     beta = (grad_sq - cross) / old_sq
     slope = grad_sq + beta * toward
-    spread.wait_send()
+    for p in range(half):
+        spread(p).wait_send()
     wait_halo(dirn, DEEP, start_send.at[4], start_recv.at[4])
     wait_halo(grad, DEEP, start_send.at[0], start_recv.at[0])
 
@@ -496,10 +502,10 @@
     @pl.loop(0, nx)
     def _(i):
         for h in range(parts):
-            dirn_s[i, :, h * LANES : (h + 1) * LANES] = dirn[i + x_lo, h, y_lo:y_hi, :]
-
-    out_dir = pltpu.make_async_copy(dirn_s, dirout_h, out_sem.at[0])
-    out_dir.start()
+            dirn_s[i, :, h * LANES : (h + 1) * LANES] = grad[i + x_lo, h, y_lo:y_hi, :]
+
+    out_grad = pltpu.make_async_copy(dirn_s, grad_h, out_sem.at[0])
+    out_grad.start()
     sample(1)
 
     @pl.loop(0, blocks)
@@ -531,35 +537,22 @@
         return tuple(s + p for s, p in zip(sums, added))
 
     sums = lax.fori_loop(0, nx, score, (zero,) * 3)
+    for i in range(nx):
+        resid_s[:, i, :] = jnp.transpose(recs[i])[:steps]
+
+    out_born = pltpu.make_async_copy(resid_s, born_h, out_sem.at[1])
+    out_born.start()
     stacked = pack(sums)
     stacked = all_sum(stacked, slots_a.at[1], gx, gxs, gx_member, 2)
-    stacked = all_sum(stacked, slots_b.at[1], place, gy_core, side_member, 3)
-    upper = shot // 2
-    stacked = all_sum(
-        stacked, slots_c, upper, shots // 2, lambda k: {"shot": k * 2 + core}, 4
-    )
+    stacked = all_sum(stacked, slots_c, wide, gys * shots, wide_member, 3)
     rec_sq, rec_res, res_sq = [unpack(stacked, k) for k in range(3)]
     length = slope / rec_sq
 
-    @pl.loop(0, nx)
-    def _(i):
-        for h in range(parts):
-            span = slice(h * LANES, (h + 1) * LANES)
-            refl[i, :, span] = refl[i, :, span] + length * dirn[i + x_lo, h, y_lo:y_hi, :]
-
-    out_image = pltpu.make_async_copy(refl, image_h, out_sem.at[1])
-    out_image.start()
-    for i in range(nx):
-        rest = traces[i + x_lo, 0, y_lo:y_hi, :] - length * recs[i]
-        resid_s[:, i, :] = jnp.transpose(rest)[:steps]
-
-    out_resid = pltpu.make_async_copy(resid_s, resid_h, out_sem.at[2])
-    out_resid.start()
     misfit = res_sq - 2.0 * length * rec_res + length * length * rec_sq
-    misfit_o[...] = jnp.broadcast_to(misfit * (0.5 / entries), (8, 128))
-    out_dir.wait()
-    out_image.wait()
-    out_resid.wait()
+    scalars = jnp.where(eight == 0, beta, jnp.where(eight == 1, length, misfit * (0.5 / entries)))
+    scalars_o[...] = scalars
+    out_grad.wait()
+    out_born.wait()
 
 
 def on_device(groups, *arguments):
@@ -578,16 +571,15 @@
     piece = pltpu.VMEM((nx // 2, parts, ny, LANES), F32)
     history = pltpu.VMEM((steps + 1, ex, parts, ey, LANES), F32)
     dma = pltpu.SemaphoreType.DMA
-    image, onward, resid, misfit = pl.pallas_call(
+    grad, born, scalars = pl.pallas_call(
         functools.partial(kernel, (nx, ny, nz, steps, entries), groups),
         out_shape=(
-            jax.ShapeDtypeStruct((nx, ny, nz), F32),
             jax.ShapeDtypeStruct((nx, ny, nz), F32),
             jax.ShapeDtypeStruct((steps, nx, ny), F32),
             jax.ShapeDtypeStruct((8, 128), F32),
         ),
-        in_specs=[whole] * 8 + [small] * 3,
-        out_specs=(whole, whole, whole, pl.BlockSpec(memory_space=pltpu.VMEM)),
+        in_specs=[whole] * 7 + [small] * 3,
+        out_specs=(whole, whole, pl.BlockSpec(memory_space=pltpu.VMEM)),
         scratch_shapes=[
             history,
             history,
@@ -607,7 +599,6 @@
             stage,
             stage,
             stage,
-            stage,
             pltpu.VMEM((steps, nx, ny), F32),
             pltpu.VMEM((nx, ny), jnp.int32),
             pltpu.VMEM((steps, nx, ny), F32),
@@ -615,25 +606,28 @@
             piece,
             piece,
             pltpu.VMEM((2, groups[1], 8, LANES), F32),
-            pltpu.VMEM((2, groups[2] * 2, 8, LANES), F32),
-            pltpu.VMEM((groups[0] // 2, 8, LANES), F32),
-            dma((8,)),
+            pltpu.VMEM((groups[2] * 2, 8, LANES), F32),
+            pltpu.VMEM((groups[2] * groups[0], 8, LANES), F32),
+            dma((7,)),
             dma((5, 8)),
             dma((5, 8)),
             dma((3, 2, 8)),
             dma((3, 2, 8)),
-            dma((3,)),
-            dma((3,)),
-            dma((5, 8)),
-            dma((5, 8)),
-            dma((3,)),
+            dma((3, nx // 2)),
+            dma((3, nx // 2)),
+            dma((4, 16)),
+            dma((4, 16)),
+            dma((2,)),
         ],
         compiler_params=pltpu.CompilerParams(
             has_side_effects=True, collective_id=0, vmem_limit_bytes=62 * 1024 * 1024
         ),
         name="iteration",
-    )(now, prev, csq, refl, dirn, oldg, residual[0], depth[0], source, wavelet, live)
-    return image, onward, resid[None], misfit[0, 0]
+    )(now, prev, csq, dirn, oldg, residual[0], depth[0], source, wavelet, live)
+    beta, length, misfit = scalars[0, 0], scalars[1, 0], scalars[2, 0]
+    onward = grad + beta * dirn
+    image = refl + length * onward
+    return image, onward, residual - length * born[None], misfit
 
 
 def solution(mesh):

time: 166 us -> 166 us (level)
  other arithmetic: 0 us -> 5.44 us
  local copies, waits for them, and re-layouts: 4.61 us -> 1.35 us
    unnamed x7 -> x6, local copies, waits for them, and re-layouts: 3.42 us -> 0.01 us
    add x0 -> x1, other arithmetic: none -> 3.34 us  [on_device(): image = refl + length * onward]
    sub x0 -> x1, other arithmetic: none -> 2.11 us  [on_device(): return (image, onward, residual - length * born[None], misfit)]
    pallas_call x1, Pallas kernels: 159 us -> 158 us  [on_device(): pl.pallas_call(functools.partial(kernel, (nx, ny, nz, steps, entries), gr...]
where the time goes in v4:
time: 166 us
  Pallas kernels  158 us (95%)
  other arithmetic  5.44 us (3%)
    pallas_call x1, Pallas kernels, on_device(): pl.pallas_call(functools.partial(kernel, (nx, ny, nz, steps, entries), gr...  158 us
    add x1, other arithmetic, on_device(): image = refl + length * onward  3.34 us

profile of v4, /device:TPU:1, one launch (start us, length us, event | category | flops | bytes accessed | tf_op | source)
XLA Modules:
  0.0 165.8 jit_solution(13746051707161964511)
XLA Ops:
  1.3 0.0 copy-start.2
  1.3 0.0 copy-start
  1.3 0.0 copy-start.1
  1.3 157.6 %iteration.1 = (f32[8,64,256]{2,1,0:T(8,128)}, f32[16,8,64]{2,1,0:T(8,128)}, f32[8,128]{1,0:T(8,128)}) custom-call(f32[8,64,256]{2,1,0:T(8,128)} %bitcast.9, f32[8,64,256]{2,1,0:T(8,128)} %bitcast.10, f32[8,64,256]{2,1,0:T(8,128)} %csq_h.1, f32[8,64,256]{2,1,0:T(8,128)} %dirn_h.1, f32[8,64,256]{2,1,0:T(8,128)} %oldg_h.1, f32[16,8,64]{2,1,0:T(8,128)} %bitcast.11, ...), custom_call_target="tpu_custom_call" | custom-call | tf_op jit(solution)/shard_map/iteration/pallas_call | solution.py:574
  159.0 1.3 fusion
  160.3 0.0 copy-done.2
  160.3 2.1 %bitcast_subtract_fusion = f32[1,16,8,64]{3,2,1,0:T(8,128)} fusion(f32[1,16,8,64]{3,2,1,0:T(8,128)S(1)} %copy-done.2, f32[16,8,64]{2,1,0:T(8,128)} %get-tuple-element.9, f32[]{:T(128)} %bitcast.4), kind=kLoop, calls=%fused_computation.2 | loop fusion | flops 16384 | bytes 98308 | tf_op jit(solution)/shard_map/sub | solution.py:630
  162.4 0.0 copy-done
  162.4 0.0 copy-done.1
  162.4 3.3 %multiply_add_fusion = (f32[8,64,256]{2,1,0:T(8,128)}, f32[8,64,256]{2,1,0:T(8,128)}) fusion(f32[8,64,256]{2,1,0:T(8,128)S(1)} %copy-done.1, f32[]{:T(128)} %bitcast.4, f32[8,64,256]{2,1,0:T(8,128)} %get-tuple-element.8, f32[8,64,256]{2,1,0:T(8,128)S(1)} %copy-done, f32[]{:T(128)} %bitcast.5), kind=kLoop, calls=%fused_computation | loop fusion | flops 524288 | bytes 2621448 | tf_op jit(solution)/shard_map/add | solution.py:629
Async XLA Ops:
  1.3 159.0 %copy-start.2 = (f32[1,16,8,64]{3,2,1,0:T(8,128)S(1)}, f32[1,16,8,64]{3,2,1,0:T(8,128)}, u32[]{:S(2)}) copy-start(f32[1,16,8,64]{3,2,1,0:T(8,128)} %param.17) | copy-start | bytes 98308
  1.3 161.1 %copy-start = (f32[8,64,256]{2,1,0:T(8,128)S(1)}, f32[8,64,256]{2,1,0:T(8,128)}, u32[]{:S(2)}) copy-start(f32[8,64,256]{2,1,0:T(8,128)} %dirn_h.1) | copy-start | bytes 1572868
  1.3 161.1 %copy-start.1 = (f32[8,64,256]{2,1,0:T(8,128)S(1)}, f32[8,64,256]{2,1,0:T(8,128)}, u32[]{:S(2)}) copy-start(f32[8,64,256]{2,1,0:T(8,128)} %param.14) | copy-start | bytes 1572868

commit v5 on v4

--- a/solution.py
+++ b/solution.py
@@ -318,29 +318,31 @@
             gain[i, h, r : r + count, :] * back[s + 1, i, h, r : r + count, :]
         )
 
-    def advance(field, s, make, send, recv):
+    def advance(field, s, make, send, recv, width):
         first, second = make(s), make(s + 1)
         target = field.at[s + 2]
         planes(field, s, x_lo - 1, x_lo + DEEP + 1, True, first)
         planes(field, s + 1, x_lo, x_lo + DEEP, False, second)
         for k in (4, 5, 0):
-            start_way(target, k, DEEP, send, recv)
+            start_way(target, k, width, send, recv)
         planes(field, s, x_hi - DEEP - 1, x_hi + 1, True, first)
         planes(field, s + 1, x_hi - DEEP, x_hi, False, second)
         for k in (6, 7, 1):
-            start_way(target, k, DEEP, send, recv)
+            start_way(target, k, width, send, recv)
         planes(field, s, x_lo + DEEP + 1, x_hi - DEEP - 1, True, first)
         planes(field, s + 1, x_lo + DEEP, x_hi - DEEP, False, second)
-        start_way(target, 2, DEEP, send, recv)
-        start_way(target, 3, DEEP, send, recv)
+        start_way(target, 2, width, send, recv)
+        start_way(target, 3, width, send, recv)
 
     blocks = (steps - 1) // 2
-
-    @pl.loop(0, blocks)
-    def _(j):
+    end = 2 * blocks + 1
+    final = (blocks - 1) % 2
+    fields = ((adj, 1, behind), (back, 0, ahead))
+
+    def both(j, width):
         s = 2 * j + 1
         now, before = lax.rem(j, 2), lax.rem(j + 1, 2)
-        for field, way, make in ((adj, 1, behind), (back, 0, ahead)):
+        for field, way, make in fields:
 
             @pl.when(j > 0)
             def _():
@@ -353,24 +355,35 @@
                     wait_halo(back.at[1], DEEP, start_send.at[2], start_recv.at[2])
                     wait_halo(back.at[0], 1, start_send.at[3], start_recv.at[3])
 
-            advance(field, s, make, halo_send.at[way, now], halo_recv.at[way, now])
-
-    end = 2 * blocks + 1
-    final = (blocks - 1) % 2
-    for field, way, make in ((adj, 1, behind), (back, 0, ahead)):
-        wait_halo(field.at[end], DEEP, halo_send.at[way, final], halo_recv.at[way, final])
+            advance(field, s, make, halo_send.at[way, now], halo_recv.at[way, now], width)
+
+    @pl.loop(0, blocks - 1)
+    def _(j):
+        both(j, DEEP)
+
+    both(jnp.int32(blocks - 1), 1)
+
+    def product(i, h, slots):
+        terms = [
+            back[a, i, h, y_lo:y_hi, :] * adj[steps + 1 - a, i, h, y_lo:y_hi, :] for a in slots
+        ]
+        return functools.reduce(lambda one, two: one + two, terms)
+
+    @pl.loop(x_lo, x_hi)
+    def _(i):
+        for h in range(parts):
+            grad[i, h, y_lo:y_hi, :] = product(i, h, range(2, steps))
+
+    for field, way, make in fields:
+        wait_halo(field.at[end], 1, halo_send.at[way, final], halo_recv.at[way, final])
         planes(field, end, x_lo, x_hi, False, make(end))
 
     start_first(4)
 
     mine, other = x_lo + half * core, x_lo + half * (1 - core)
 
-    def product(i, h):
-        total = back[1, i, h, y_lo:y_hi, :] * adj[steps, i, h, y_lo:y_hi, :]
-        for a in range(2, steps + 1):
-            one, two = back[a, i, h, y_lo:y_hi, :], adj[steps + 1 - a, i, h, y_lo:y_hi, :]
-            total = total + one * two
-        return total
+    def complete(i, h):
+        return grad[i, h, y_lo:y_hi, :] + product(i, h, (1, steps))
 
     def pair_copy(src, dst, k, p, device):
         return pltpu.make_async_remote_copy(
@@ -401,13 +414,13 @@
     @pl.loop(0, half)
     def _(p):
         for h in range(parts):
-            half_c[p, h] = product(other + p, h)
+            half_c[p, h] = complete(other + p, h)
         swap_a(p).start()
 
     @pl.loop(0, half)
     def _(p):
         for h in range(parts):
-            grad[mine + p, h, y_lo:y_hi, :] = product(mine + p, h)
+            grad[mine + p, h, y_lo:y_hi, :] = complete(mine + p, h)
         swap_a(p).wait()
         add_plane(p, half_a)
         swap_b(p).start()
@@ -508,8 +521,7 @@
     out_grad.start()
     sample(1)
 
-    @pl.loop(0, blocks)
-    def _(j):
+    def born(j, width):
         s = 2 * j + 1
         now, before = lax.rem(j, 2), lax.rem(j + 1, 2)
 
@@ -517,11 +529,16 @@
         def _():
             wait_halo(adj.at[s], DEEP, halo_send.at[2, before], halo_recv.at[2, before])
 
-        advance(adj, s, scattered, halo_send.at[2, now], halo_recv.at[2, now])
+        advance(adj, s, scattered, halo_send.at[2, now], halo_recv.at[2, now], width)
         sample(s + 1)
         sample(s + 2)
 
-    wait_halo(adj.at[end], DEEP, halo_send.at[2, final], halo_recv.at[2, final])
+    @pl.loop(0, blocks - 1)
+    def _(j):
+        born(j, DEEP)
+
+    born(jnp.int32(blocks - 1), 1)
+    wait_halo(adj.at[end], 1, halo_send.at[2, final], halo_recv.at[2, final])
     planes(adj, end, x_lo, x_hi, False, scattered(end))
     sample(end + 1)
 
@@ -553,6 +570,21 @@
     scalars_o[...] = scalars
     out_grad.wait()
     out_born.wait()
+
+
+def finish(scalars, grad, dirn, refl, residual, born, image, onward, resid, misfit):
+    beta, length = scalars[0:1, 0:1], scalars[1:2, 0:1]
+    misfit[0, 0] = jnp.sum(scalars[2:3, 0:1])
+
+    @pl.loop(0, grad.shape[0])
+    def _(i):
+        path = grad[i] + beta * dirn[i]
+        onward[i] = path
+        image[i] = refl[i] + length * path
+
+    @pl.loop(0, residual.shape[0])
+    def _(n):
+        resid[n] = residual[n] - length * born[n]
 
 
 def on_device(groups, *arguments):
@@ -624,10 +656,20 @@
         ),
         name="iteration",
     )(now, prev, csq, dirn, oldg, residual[0], depth[0], source, wavelet, live)
-    beta, length, misfit = scalars[0, 0], scalars[1, 0], scalars[2, 0]
-    onward = grad + beta * dirn
-    image = refl + length * onward
-    return image, onward, residual - length * born[None], misfit
+    vector = pl.BlockSpec(memory_space=pltpu.VMEM)
+    image, onward, resid, misfit = pl.pallas_call(
+        finish,
+        out_shape=(
+            jax.ShapeDtypeStruct((nx, ny, nz), F32),
+            jax.ShapeDtypeStruct((nx, ny, nz), F32),
+            jax.ShapeDtypeStruct((steps, nx, ny), F32),
+            jax.ShapeDtypeStruct((1, 1), F32),
+        ),
+        in_specs=[vector] * 6,
+        out_specs=(vector, vector, vector, small),
+        name="finish",
+    )(scalars, grad, dirn, refl, residual[0], born)
+    return image, onward, resid[None], misfit[0, 0]
 
 
 def solution(mesh):

time: 166 us -> 159 us (0.958)
  other arithmetic: 5.44 us -> 0 us
    add x1 -> x0, other arithmetic: 3.34 us -> none  [on_device(): image = refl + length * onward]
    pallas_call x0 -> x1, Pallas kernels: none -> 2.86 us  [on_device(): pl.pallas_call(finish, out_shape=(jax.ShapeDtypeStruct((nx, ny, nz), F32)...]
    pallas_call x1, Pallas kernels: 158 us -> 155 us  [on_device(): pl.pallas_call(functools.partial(kernel, (nx, ny, nz, steps, entries), gr...]
    sub x1 -> x0, other arithmetic: 2.11 us -> none  [on_device(): return (image, onward, residual - length * born[None], misfit)]
where the time goes in v5:
time: 159 us
  Pallas kernels  158 us (99%)
    pallas_call x1, Pallas kernels, on_device(): pl.pallas_call(functools.partial(kernel, (nx, ny, nz, steps, entries), gr...  155 us

profile of v5, /device:TPU:1, one launch (start us, length us, event | category | flops | bytes accessed | tf_op | source)
XLA Modules:
  0.0 159.3 jit_solution(480296231119163127)
XLA Ops:
  1.3 155.1 %iteration.1 = (f32[8,64,256]{2,1,0:T(8,128)}, f32[16,8,64]{2,1,0:T(8,128)}, f32[8,128]{1,0:T(8,128)}) custom-call(f32[8,64,256]{2,1,0:T(8,128)} %bitcast.6, f32[8,64,256]{2,1,0:T(8,128)} %bitcast.7, f32[8,64,256]{2,1,0:T(8,128)} %csq_h.1, f32[8,64,256]{2,1,0:T(8,128)} %dirn.1, f32[8,64,256]{2,1,0:T(8,128)} %oldg_h.1, f32[16,8,64]{2,1,0:T(8,128)} %bitcast.8, ...), custom_call_target="tpu_custom_call" | custom-call | tf_op jit(solution)/shard_map/iteration/pallas_call | solution.py:606
  156.4 2.9 %finish.1 = (f32[8,64,256]{2,1,0:T(8,128)}, f32[8,64,256]{2,1,0:T(8,128)}, f32[16,8,64]{2,1,0:T(8,128)}, f32[1,1]{1,0:T(1,128)}) custom-call(f32[8,128]{1,0:T(8,128)} %get-tuple-element.11.scalars, f32[8,64,256]{2,1,0:T(8,128)} %get-tuple-element.12.grad, f32[8,64,256]{2,1,0:T(8,128)} %dirn.1, f32[8,64,256]{2,1,0:T(8,128)} %refl.1, f32[16,8,64]{2,1,0:T(8,128)} %bitcast.9, ...), custom_call_target="tpu_custom_call" | custom-call | tf_op jit(solution)/shard_map/finish/pallas_call | solution.py:660

commit v6 on v5

--- a/solution.py
+++ b/solution.py
@@ -99,8 +99,11 @@
             (pl.ds(*dst_x), slice(None), pl.ds(*dst_y), slice(None)),
         )
 
+    def depth_of(k, width):
+        return width if k < 4 else 1
+
     def halo_copy(ref, k, width, send, recv):
-        src, dst = regions(WAYS[k], width)
+        src, dst = regions(WAYS[k], depth_of(k, width))
         return pltpu.make_async_remote_copy(
             src_ref=ref.at[src],
             dst_ref=ref.at[dst],
@@ -115,12 +118,16 @@
         def _():
             halo_copy(ref, k, width, send, recv).start()
 
+    def used(width):
+        return (4, 5, 6, 7, 0, 1, 2, 3) if width == DEEP else (0, 1, 2, 3)
+
     def start_halo(ref, width, send, recv):
-        for k in (4, 5, 6, 7, 0, 1, 2, 3):
+        for k in used(width):
             start_way(ref, k, width, send, recv)
 
     def wait_halo(ref, width, send, recv):
-        for k, way in enumerate(WAYS):
+        for k in used(width):
+            way = WAYS[k]
             came = has((-way[0], -way[1]))
 
             @pl.when(came)
@@ -129,7 +136,7 @@
 
             @pl.when(jnp.logical_not(came))
             def _():
-                where = regions(way, width)[1]
+                where = regions(way, depth_of(k, width))[1]
                 view = ref.at[where]
                 view[...] = jnp.zeros(view.shape, F32)
 
@@ -301,7 +308,7 @@
             strip(field, s, i, y_hi, TILE, extra)
 
     def planes(field, s, lo, hi, whole, extra):
-        @pl.loop(lo, hi, unroll=2)
+        @pl.loop(lo, hi, unroll=3 if (hi - lo) % 2 else 2)
         def _(i):
             plane(field, s, i, whole, extra)
 
@@ -321,18 +328,28 @@
     def advance(field, s, make, send, recv, width):
         first, second = make(s), make(s + 1)
         target = field.at[s + 2]
-        planes(field, s, x_lo - 1, x_lo + DEEP + 1, True, first)
-        planes(field, s + 1, x_lo, x_lo + DEEP, False, second)
-        for k in (4, 5, 0):
-            start_way(target, k, width, send, recv)
-        planes(field, s, x_hi - DEEP - 1, x_hi + 1, True, first)
-        planes(field, s + 1, x_hi - DEEP, x_hi, False, second)
-        for k in (6, 7, 1):
-            start_way(target, k, width, send, recv)
-        planes(field, s, x_lo + DEEP + 1, x_hi - DEEP - 1, True, first)
-        planes(field, s + 1, x_lo + DEEP, x_hi - DEEP, False, second)
-        start_way(target, 2, width, send, recv)
-        start_way(target, 3, width, send, recv)
+        left, right = x_lo, x_hi - 1
+
+        def go(*ways):
+            for k in ways:
+                if k in used(width):
+                    start_way(target, k, width, send, recv)
+
+        planes(field, s, left - 1, left + 2, True, first)
+        plane(field, s + 1, left, False, second)
+        go(4, 5)
+        planes(field, s, right - 1, right + 2, True, first)
+        plane(field, s + 1, right, False, second)
+        go(6, 7)
+        plane(field, s, left + 2, True, first)
+        plane(field, s + 1, left + 1, False, second)
+        go(0)
+        plane(field, s, right - 2, True, first)
+        plane(field, s + 1, right - 1, False, second)
+        go(1)
+        planes(field, s, left + 3, right - 2, True, first)
+        planes(field, s + 1, left + 2, right - 1, False, second)
+        go(2, 3)
 
     blocks = (steps - 1) // 2
     end = 2 * blocks + 1

time: 159 us -> 153 us (0.962)
  Pallas kernels: 158 us -> 152 us
    pallas_call x1, Pallas kernels: 155 us -> 149 us  [on_device(): pl.pallas_call(functools.partial(kernel, (nx, ny, nz, steps, entries), gr...]
where the time goes in v6:
time: 153 us
  Pallas kernels  152 us (99%)
    pallas_call x1, Pallas kernels, on_device(): pl.pallas_call(functools.partial(kernel, (nx, ny, nz, steps, entries), gr...  149 us

profile of v6, /device:TPU:1, one launch (start us, length us, event | category | flops | bytes accessed | tf_op | source)
XLA Modules:
  0.0 153.2 jit_solution(3402378127419054254)
XLA Ops:
  1.3 149.1 %iteration.1 = (f32[8,64,256]{2,1,0:T(8,128)}, f32[16,8,64]{2,1,0:T(8,128)}, f32[8,128]{1,0:T(8,128)}) custom-call(f32[8,64,256]{2,1,0:T(8,128)} %bitcast.6, f32[8,64,256]{2,1,0:T(8,128)} %bitcast.7, f32[8,64,256]{2,1,0:T(8,128)} %csq_h.1, f32[8,64,256]{2,1,0:T(8,128)} %dirn.1, f32[8,64,256]{2,1,0:T(8,128)} %oldg_h.1, f32[16,8,64]{2,1,0:T(8,128)} %bitcast.8, ...), custom_call_target="tpu_custom_call" | custom-call | tf_op jit(solution)/shard_map/iteration/pallas_call | solution.py:623
  150.4 2.9 %finish.1 = (f32[8,64,256]{2,1,0:T(8,128)}, f32[8,64,256]{2,1,0:T(8,128)}, f32[16,8,64]{2,1,0:T(8,128)}, f32[1,1]{1,0:T(1,128)}) custom-call(f32[8,128]{1,0:T(8,128)} %get-tuple-element.11.scalars, f32[8,64,256]{2,1,0:T(8,128)} %get-tuple-element.12.grad, f32[8,64,256]{2,1,0:T(8,128)} %dirn.1, f32[8,64,256]{2,1,0:T(8,128)} %refl.1, f32[16,8,64]{2,1,0:T(8,128)} %bitcast.9, ...), custom_call_target="tpu_custom_call" | custom-call | tf_op jit(solution)/shard_map/finish/pallas_call | solution.py:677

commit v7 on v6

--- a/solution.py
+++ b/solution.py
@@ -125,8 +125,8 @@
         for k in used(width):
             start_way(ref, k, width, send, recv)
 
-    def wait_halo(ref, width, send, recv):
-        for k in used(width):
+    def wait_halo(ref, width, send, recv, ways=range(8)):
+        for k in [k for k in used(width) if k in ways]:
             way = WAYS[k]
             came = has((-way[0], -way[1]))
 
@@ -143,6 +143,51 @@
             @pl.when(has(way))
             def _():
                 halo_copy(ref, k, width, send, recv).wait_send()
+
+    def side_copy(ref, t, dy, width, send, recv):
+        src_y, dst_y = {
+            -1: ((y_lo, TILE), (y_hi, TILE)),
+            1: ((y_hi - TILE, TILE), (0, TILE)),
+            0: ((y_lo, ny), (y_lo, ny)),
+        }[dy]
+        deep = width if dy == 0 else 1
+        k = t if dy == 0 else 4 + 2 * t + (dy + 1) // 2
+        src = (pl.ds(x_lo + t * (nx - deep), deep), slice(None), pl.ds(*src_y), slice(None))
+        dst = (pl.ds(x_hi - t * (nx + deep), deep), slice(None), pl.ds(*dst_y), slice(None))
+        if send is None:
+            return ref.at[dst]
+        return pltpu.make_async_remote_copy(
+            src_ref=ref.at[src],
+            dst_ref=ref.at[dst],
+            send_sem=send.at[k],
+            recv_sem=recv.at[k],
+            device_id={"gx": gx + 2 * t - 1, "gy": gy + dy},
+            device_id_type=MESH,
+        )
+
+    def start_side(ref, t, dys, width, send, recv):
+        for dy in dys:
+
+            @pl.when(has((2 * t - 1, dy)))
+            def _():
+                side_copy(ref, t, dy, width, send, recv).start()
+
+    def wait_side(ref, t, width, send, recv):
+        for dy in (0, -1, 1):
+            came = has((1 - 2 * t, -dy))
+
+            @pl.when(came)
+            def _():
+                side_copy(ref, t, dy, width, send, recv).wait_recv()
+
+            @pl.when(jnp.logical_not(came))
+            def _():
+                view = side_copy(ref, t, dy, width, None, None)
+                view[...] = jnp.zeros(view.shape, F32)
+
+            @pl.when(has((2 * t - 1, dy)))
+            def _():
+                side_copy(ref, t, dy, width, send, recv).wait_send()
 
     xs, ys = pl.ds(x_lo, nx), pl.ds(y_lo, ny)
 
@@ -303,7 +348,8 @@
     def plane(field, s, i, whole, extra):
         if whole:
             strip(field, s, i, 0, TILE, extra)
-        strip(field, s, i, y_lo, ny, extra)
+        for r in range(y_lo, y_hi, 16):
+            strip(field, s, i, r, 16, extra)
         if whole:
             strip(field, s, i, y_hi, TILE, extra)
 
@@ -325,31 +371,39 @@
             gain[i, h, r : r + count, :] * back[s + 1, i, h, r : r + count, :]
         )
 
-    def advance(field, s, make, send, recv, width):
+    def advance(field, s, make, j, sends, recvs, width):
         first, second = make(s), make(s + 1)
+        now, before = lax.rem(j, 2), lax.rem(j + 1, 2)
+        send, recv = sends.at[now], recvs.at[now]
         target = field.at[s + 2]
         left, right = x_lo, x_hi - 1
 
-        def go(*ways):
-            for k in ways:
-                if k in used(width):
-                    start_way(target, k, width, send, recv)
-
-        planes(field, s, left - 1, left + 2, True, first)
-        plane(field, s + 1, left, False, second)
-        go(4, 5)
-        planes(field, s, right - 1, right + 2, True, first)
-        plane(field, s + 1, right, False, second)
-        go(6, 7)
-        plane(field, s, left + 2, True, first)
-        plane(field, s + 1, left + 1, False, second)
-        go(0)
-        plane(field, s, right - 2, True, first)
-        plane(field, s + 1, right - 1, False, second)
-        go(1)
+        @pl.when(j > 0)
+        def _():
+            wait_halo(field.at[s], DEEP, sends.at[before], recvs.at[before], (2, 3))
+
+        for t in (before, now):
+
+            @pl.when(j > 0)
+            def _():
+                wait_side(field.at[s], 1 - t, DEEP, sends.at[before], recvs.at[before])
+
+            near, inward = left + t * (nx - 1), 1 - 2 * t
+
+            @pl.loop(0, 3, unroll=3)
+            def _(i):
+                plane(field, s, near - 1 + i, True, first)
+
+            plane(field, s + 1, near, False, second)
+            if width == DEEP:
+                start_side(target, t, (-1, 1), width, send, recv)
+            plane(field, s, near + 2 * inward, True, first)
+            plane(field, s + 1, near + inward, False, second)
+            start_side(target, t, (0,), width, send, recv)
         planes(field, s, left + 3, right - 2, True, first)
         planes(field, s + 1, left + 2, right - 1, False, second)
-        go(2, 3)
+        start_way(target, 2, width, send, recv)
+        start_way(target, 3, width, send, recv)
 
     blocks = (steps - 1) // 2
     end = 2 * blocks + 1
@@ -358,13 +412,7 @@
 
     def both(j, width):
         s = 2 * j + 1
-        now, before = lax.rem(j, 2), lax.rem(j + 1, 2)
         for field, way, make in fields:
-
-            @pl.when(j > 0)
-            def _():
-                wait_halo(field.at[s], DEEP, halo_send.at[way, before], halo_recv.at[way, before])
-
             if way == 0:
 
                 @pl.when(j == 0)
@@ -372,7 +420,7 @@
                     wait_halo(back.at[1], DEEP, start_send.at[2], start_recv.at[2])
                     wait_halo(back.at[0], 1, start_send.at[3], start_recv.at[3])
 
-            advance(field, s, make, halo_send.at[way, now], halo_recv.at[way, now], width)
+            advance(field, s, make, j, halo_send.at[way], halo_recv.at[way], width)
 
     @pl.loop(0, blocks - 1)
     def _(j):
@@ -540,13 +588,7 @@
 
     def born(j, width):
         s = 2 * j + 1
-        now, before = lax.rem(j, 2), lax.rem(j + 1, 2)
-
-        @pl.when(j > 0)
-        def _():
-            wait_halo(adj.at[s], DEEP, halo_send.at[2, before], halo_recv.at[2, before])
-
-        advance(adj, s, scattered, halo_send.at[2, now], halo_recv.at[2, now], width)
+        advance(adj, s, scattered, j, halo_send.at[2], halo_recv.at[2], width)
         sample(s + 1)
         sample(s + 2)
 
@@ -673,7 +715,10 @@
         ),
         name="iteration",
     )(now, prev, csq, dirn, oldg, residual[0], depth[0], source, wavelet, live)
-    vector = pl.BlockSpec(memory_space=pltpu.VMEM)
+    few = 2
+    vector = pl.BlockSpec((8, LANES), lambda i: (0, 0))
+    cube = pl.BlockSpec((nx // few, ny, nz), lambda i: (i, 0, 0))
+    trace = pl.BlockSpec((steps // few, nx, ny), lambda i: (i, 0, 0))
     image, onward, resid, misfit = pl.pallas_call(
         finish,
         out_shape=(
@@ -682,8 +727,9 @@
             jax.ShapeDtypeStruct((steps, nx, ny), F32),
             jax.ShapeDtypeStruct((1, 1), F32),
         ),
-        in_specs=[vector] * 6,
-        out_specs=(vector, vector, vector, small),
+        grid=(few,),
+        in_specs=[vector, cube, cube, cube, trace, trace],
+        out_specs=(cube, cube, trace, small),
         name="finish",
     )(scalars, grad, dirn, refl, residual[0], born)
     return image, onward, resid[None], misfit[0, 0]

time: 153 us -> 151 us (0.987)
  Pallas kernels: 152 us -> 149 us
    pallas_call x1, Pallas kernels: 149 us -> 147 us  [on_device(): pl.pallas_call(functools.partial(kernel, (nx, ny, nz, steps, entries), gr...]
where the time goes in v7:
time: 151 us
  Pallas kernels  149 us (99%)
    pallas_call x1, Pallas kernels, on_device(): pl.pallas_call(functools.partial(kernel, (nx, ny, nz, steps, entries), gr...  147 us

profile of v7, /device:TPU:1, one launch (start us, length us, event | category | flops | bytes accessed | tf_op | source)
XLA Modules:
  0.0 150.7 jit_solution(3544148345527705264)
XLA Ops:
  1.3 146.9 %iteration.1 = (f32[8,64,256]{2,1,0:T(8,128)}, f32[16,8,64]{2,1,0:T(8,128)}, f32[8,128]{1,0:T(8,128)}) custom-call(f32[8,64,256]{2,1,0:T(8,128)} %bitcast.6, f32[8,64,256]{2,1,0:T(8,128)} %bitcast.7, f32[8,64,256]{2,1,0:T(8,128)} %csq_h.1, f32[8,64,256]{2,1,0:T(8,128)} %dirn.1, f32[8,64,256]{2,1,0:T(8,128)} %oldg_h.1, f32[16,8,64]{2,1,0:T(8,128)} %bitcast.8, ...), custom_call_target="tpu_custom_call" | custom-call | tf_op jit(solution)/shard_map/iteration/pallas_call | solution.py:665
  148.2 2.6 %finish.1 = (f32[8,64,256]{2,1,0:T(8,128)}, f32[8,64,256]{2,1,0:T(8,128)}, f32[16,8,64]{2,1,0:T(8,128)}, f32[1,1]{1,0:T(1,128)}) custom-call(f32[8,128]{1,0:T(8,128)} %get-tuple-element.11.scalars, f32[8,64,256]{2,1,0:T(8,128)} %get-tuple-element.12.grad, f32[8,64,256]{2,1,0:T(8,128)} %dirn.1, f32[8,64,256]{2,1,0:T(8,128)} %refl.1, f32[16,8,64]{2,1,0:T(8,128)} %bitcast.9, ...), custom_call_target="tpu_custom_call" | custom-call | tf_op jit(solution)/shard_map/finish/pallas_call | solution.py:722
